TPU v7x, 32 devices: a whole 2x2x4 slice. The times are simulated.
32 devices in a mesh: dom: 8 (over y, x, core), band: 4 (over z).
Axes of the slice: x: 2, y: 2, z: 4, core: 2. Of those that a mesh axis runs over, the one named last changes fastest.
Arguments:
- orbitals: bfloat16 [768, 8, 6, 1152], P('band', 'dom'), may hold values from -6 to 6
- occupations: float32 [768], P('band'), may hold values from 0.2 to 2
- previous: float32 [8, 12, 4608], P('dom'), may hold values from -6 to 6
- compensation: float32 [8, 12, 4608], P('dom'), may hold values from 0 to 1.5
- local_potential: float32 [8, 6, 1152], P('dom'), may hold values from -6 to 6
Outputs:
- applied: bfloat16 [768, 8, 6, 1152], P('band', 'dom')
- potential: float32 [8, 12, 4608], P('dom')
All inputs are finite; a program needn't handle non-finite values.
Results may differ from a plain program's by a relative error of at most 0.001.
Values may be sent and summed in bfloat16 or wider, within the bound.
No kernel may reach another device: no remote copies, remote signals or barrier semaphores. Data moves between devices by JAX's collectives and lax.ppermute only.
A program may use at most 64 MiB of HBM per device.

v0:
```python
import functools
import math

import jax
import jax.numpy as jnp
import numpy as np
from jax import lax
from jax.experimental import pallas as pl
from jax.experimental.pallas import tpu as pltpu
from jax.sharding import PartitionSpec as P


BY = 24
BZ = 48
SWEEPS = 4

F32, BF16 = jnp.float32, jnp.bfloat16
LANES = 128
PAD = 8
ZOFF = 16
WV = SWEEPS + 1
WS = SWEEPS
WC = WS // 2 + 1


def sides(count):
    return ("swap",) if count == 2 else ("lo", "hi")


def fetch(block, counts, moves):
    pairs = []
    for target in np.ndindex(*counts):
        source = list(target)
        for axis, side in moves.items():
            source[axis] = {"swap": 1 - target[axis], "lo": target[axis] - 1, "hi": target[axis] + 1}[side]
        if all(0 <= s < n for s, n in zip(source, counts)):
            pairs.append((int(np.ravel_multi_index(source, counts)), int(np.ravel_multi_index(target, counts))))
    return lax.ppermute(block, "dom", pairs)


def rim_start(side, coord, length, width):
    if side == "swap":
        return jnp.where(coord == 0, length - width, 0)
    return length - width if side == "lo" else 0


def halo_start(side, coord, low, high):
    if side == "swap":
        return jnp.where(coord == 0, high, low)
    return low if side == "lo" else high


def position(counts):
    at = lax.axis_index("dom")
    return at // (counts[1] * counts[2]), at // counts[2] % counts[1], at % counts[2]


def lane_iota(rows):
    return lax.broadcasted_iota(jnp.int32, (rows, LANES), 1)


def exact_dot(value, weights):
    high = value.astype(BF16)
    rest = value - high.astype(F32)
    middle = rest.astype(BF16)
    low = (rest - middle.astype(F32)).astype(BF16)
    dot = functools.partial(jnp.dot, preferred_element_type=F32)
    return dot(high, weights) + (dot(middle, weights) + dot(low, weights))


def grid2(rows, columns):
    shape = (rows, columns)
    return (lax.broadcasted_iota(jnp.int32, shape, d) for d in (0, 1))


def z_refine(core):
    cell, lane = grid2(LANES, LANES)
    fine = lane - ZOFF + 2 * BZ * core
    here = fine >> 1
    other = here + 2 * (fine & 1) - 1
    return jnp.where(cell == here, 0.75, jnp.where(cell == other, 0.25, 0.0)).astype(BF16)


def z_coarsen():
    lane, cell = grid2(LANES, LANES)
    step = lane - ZOFF - 2 * cell
    w = jnp.where((step == 0) | (step == 1), 0.375, jnp.where((step == -1) | (step == 2), 0.125, 0.0))
    return jnp.where(cell < BZ, w, 0.0).astype(BF16)


def z_pick(core):
    lane, y = grid2(BY * BZ, LANES)
    return jnp.where(lane == BZ * y + jnp.where(core == 0, BZ - 1, 0), 1.0, 0.0).astype(BF16)


def z_spread(core):
    y, lane = grid2(LANES, BY * BZ)
    return jnp.where(lane == BZ * y + jnp.where(core == 0, BZ - 1, 0), -0.5, 0.0).astype(BF16)


def stencil(first, columns):
    source, lane = grid2(4 * LANES, columns)
    step = source - LANES - lane
    z = (lax.broadcasted_iota(jnp.int32, (1, columns), 1) + first) % BZ
    up = jnp.where(z == BZ - 1, 2 * BY * BZ, 1)
    down = jnp.where(z == 0, 2 * BY * BZ, -1)
    near = (step == up) | (step == down) | (step == BZ) | (step == -BZ)
    return jnp.where(near, -0.5, jnp.where(step == 0, 3.0, 0.0)).astype(BF16)


def sum_rows(value):
    while value.shape[0] % 16 == 0:
        half = value.shape[0] // 2
        value = value[:half] + value[half:]
    return jnp.sum(value, axis=0, keepdims=True)


def density_kernel(counts, orb, occ, part, held, zf, *refs):
    x_faces, (weights, load, load_occ) = refs[:-3], refs[-3:]
    planes, bands, width = held.shape
    tiles = width // LANES
    pos = position(counts)
    first = pltpu.make_async_copy(occ, weights, load_occ)
    first.start()
    loads = [pltpu.make_async_copy(orb.at[x], held.at[x], load.at[x]) for x in range(planes)]
    for copy in loads:
        copy.start()
    pick = z_pick(pos[2])
    first.wait()
    rows = jnp.broadcast_to(weights[...], (LANES, bands))
    rows = jnp.concatenate([rows, jnp.zeros((LANES, -bands % LANES), F32)], 1)
    weight = jnp.concatenate([rows[:, b : b + LANES].T for b in range(0, bands, LANES)], 0)[:bands]
    for x in range(planes):
        loads[x].wait()
        for t in range(tiles):
            f = held[x, :, t * LANES : (t + 1) * LANES].astype(F32)
            part[tiles * x + t : tiles * x + t + 1, :] = sum_rows(f * f * weight)
        zf[x] = jnp.dot(held[x], pick, preferred_element_type=F32).astype(BF16)
    for side, face in zip(sides(counts[0]), x_faces):
        face[...] = held[rim_start(side, pos[0], planes, 1)]


def total_kernel(counts, scale, *refs):
    parts, out, flat = refs[:-2], refs[-2], refs[-1]
    total = parts[0][...]
    for part in parts[1:]:
        total = total + part[...]
    flat[...] = total * scale
    per = 384 // BZ
    groups = flat.shape[0] // 3
    lane = lane_iota(groups)
    shift = jnp.where(position(counts)[2] == 0, 0, BZ)
    tile = [flat[pl.ds(j, groups, stride=3), :] for j in range(3)]
    for k in range(per):
        at, off = divmod(BZ * k, LANES)
        row = pltpu.roll(tile[at], (LANES - off) % LANES, 1) if off else tile[at]
        if off + BZ > LANES:
            row = jnp.where(lane < LANES - off, row, pltpu.roll(tile[at + 1], LANES - off, 1))
        row = jnp.where(lane < BZ, row, 0.0)
        out[pl.ds(k, groups, stride=per), :] = pltpu.roll(row, shift, 1)


def cut_kernel(counts, rho, mate, chip, *sends):
    cx, cy, _ = position(counts)
    chip[...] = rho[...] + mate[...]
    sends = list(sends)
    x_sides, y_sides = sides(counts[0]), sides(counts[1])
    bx = chip.shape[0] // BY
    for side in x_sides:
        at = pl.multiple_of(BY * rim_start(side, cx, bx, WC), 8)
        sends.pop(0)[...] = chip[pl.ds(at, WC * BY), :].astype(BF16)
    for side in y_sides:
        at = rim_start(side, cy, BY, PAD)
        rows = [chip[pl.ds(pl.multiple_of(BY * x + at, 8), PAD), :] for x in range(bx)]
        sends.pop(0)[...] = jnp.concatenate(rows, 0).astype(BF16)
    for x_side in x_sides:
        for y_side in y_sides:
            at_x, at = rim_start(x_side, cx, bx, WC), rim_start(y_side, cy, BY, PAD)
            rows = [chip[pl.ds(pl.multiple_of(BY * (at_x + x) + at, 8), PAD), :] for x in range(WC)]
            rows.append(jnp.zeros((PAD, LANES), F32))
            sends.pop(0)[...] = jnp.concatenate(rows, 0).astype(BF16)


def field_rows(ref, groups):
    lane = lane_iota(groups)
    a, b, c = (ref[pl.ds(j, groups, stride=3), :] for j in range(3))
    return (
        pltpu.roll(a, 16, 1),
        jnp.where(lane < 48, pltpu.roll(a, 48, 1), pltpu.roll(b, 48, 1)),
        jnp.where(lane < 80, pltpu.roll(b, 80, 1), pltpu.roll(c, 80, 1)),
        pltpu.roll(c, 112, 1),
    )


def field_kernel(counts, orb, prev, comp, mate_prev, mate_comp, ext, *refs):
    sends, pos = list(refs), position(counts)
    bx, bands, row_lanes = orb.shape
    half = bands // 2
    fx, fy = prev.shape[0] * LANES // (2 * BY * 2 * BZ), 2 * BY
    groups = prev.shape[0] // 3
    lane = lane_iota(groups)
    own = (lane >= ZOFF) & (lane < ZOFF + 2 * BZ)
    first = pos[2] == 0
    shift = jnp.where(first, 2 * BZ, LANES - 2 * BZ)
    edge_low = jnp.where(first, ZOFF + 2 * BZ, 0)
    edge_high = jnp.where(first, LANES, ZOFF)
    edge = (lane >= edge_low) & (lane < edge_high)
    rows = fx * fy
    for f, (ref, mate) in enumerate(((prev, mate_prev), (comp, mate_comp))):
        mine = field_rows(ref, groups)
        theirs = field_rows(mate, groups)
        for k in range(4):
            halo = jnp.where(edge, pltpu.roll(theirs[k], shift, 1), 0.0)
            ext[pl.ds(f * rows + k, groups, stride=4), :] = jnp.where(own, mine[k], halo)
    widths = (WV, WS)
    x_sides, y_sides = sides(counts[0]), sides(counts[1])
    for side in x_sides:
        send, done = sends.pop(0), 0
        for f, width in enumerate(widths):
            start = f * rows + fy * rim_start(side, pos[0], fx, width)
            send[pl.ds(done, width * fy), :] = ext[pl.ds(pl.multiple_of(start, 8), width * fy), :].astype(BF16)
            done += width * fy
    first_half = lane_iota(half) < BZ
    for side in y_sides:
        send = sends.pop(0)
        start = pl.multiple_of(rim_start(side, pos[1], row_lanes, LANES), LANES)
        turn = jnp.where(pos[1] == 0, BZ, 0) if side == "swap" else (BZ if side == "lo" else 0)
        for x in range(bx):
            face = orb[x, :, pl.ds(start, LANES)].astype(F32)
            both = jnp.where(first_half, pltpu.roll(face[:half], turn, 1), pltpu.roll(face[half:], turn + BZ, 1))
            send[pl.ds(x * half, half), :] = both.astype(BF16)
        at = rim_start(side, pos[1], fy, PAD)
        for f in range(2):
            cut = [ext[pl.ds(pl.multiple_of(f * rows + fy * x + at, 8), PAD), :] for x in range(fx)]
            send[pl.ds(bx * half + f * fx * PAD, fx * PAD), :] = jnp.concatenate(cut, 0).astype(BF16)
    for x_side in x_sides:
        for y_side in y_sides:
            send = sends.pop(0)
            at = rim_start(y_side, pos[1], fy, PAD)
            cut = []
            for f, width in enumerate(widths):
                start = rim_start(x_side, pos[0], fx, width)
                cut += [
                    ext[pl.ds(pl.multiple_of(f * rows + fy * (start + x) + at, 8), PAD), :]
                    for x in range(width)
                ]
            cut.append(jnp.zeros((PAD, LANES), F32))
            send[...] = jnp.concatenate(cut, 0).astype(BF16)


def finish_kernel(counts, *refs):
    it = iter(refs)
    chip, ext, local_potential, orb, inner, zf = (next(it) for _ in range(6))
    x_sides, y_sides = sides(counts[0]), sides(counts[1])
    xy_sides = [(a, b) for a in x_sides for b in y_sides]
    rho_x, rho_y, rho_xy = ([next(it) for _ in s] for s in (x_sides, y_sides, xy_sides))
    fld_x, fld_y, fld_xy = ([next(it) for _ in s] for s in (x_sides, y_sides, xy_sides))
    x_faces = [next(it) for _ in x_sides]
    out, potential_out = next(it), next(it)
    coarse, wide, fine, v0, v1, src, flat, effective, potential, result, store, store_potential = it
    cx, cy, cz = position(counts)
    bands = orb.shape[1]
    bx = chip.shape[0] // BY
    fx, fy = 2 * bx, 2 * BY
    ry, rc = fy + 2 * PAD, BY + 2 * PAD
    qx = fx + 2 * WV
    face_rows = bx * bands // 2

    coarse[...] = jnp.zeros_like(coarse)
    for x in range(bx):
        coarse[WC + x, PAD : PAD + BY, :] = chip[x * BY : (x + 1) * BY, :]
    for side, ref in zip(x_sides, rho_x):
        at = halo_start(side, cx, 0, WC + bx)
        block = ref[...].astype(F32)
        for x in range(WC):
            coarse[at + x, PAD : PAD + BY, :] = block[x * BY : (x + 1) * BY, :]
    for side, ref in zip(y_sides, rho_y):
        at = pl.multiple_of(halo_start(side, cy, 0, PAD + BY), 8)
        block = ref[...].astype(F32)
        for x in range(bx):
            coarse[WC + x, pl.ds(at, PAD), :] = block[x * PAD : (x + 1) * PAD, :]
    for (x_side, y_side), ref in zip(xy_sides, rho_xy):
        at_x = halo_start(x_side, cx, 0, WC + bx)
        at = pl.multiple_of(halo_start(y_side, cy, 0, PAD + BY), 8)
        block = ref[...].astype(F32)
        for x in range(WC):
            coarse[at_x + x, pl.ds(at, PAD), :] = block[x * PAD : (x + 1) * PAD, :]

    v0[...] = jnp.zeros_like(v0)
    src[...] = jnp.zeros_like(src)
    for f, (ref, width) in enumerate(((v0, WV), (src, WS))):
        rows = f * fx * fy
        for x in range(fx):
            ref[WV + x, PAD : PAD + fy, :] = ext[rows + x * fy : rows + (x + 1) * fy, :]
        done = f * WV
        for side, got in zip(x_sides, fld_x):
            at = halo_start(side, cx, WV - width, WV + fx)
            for x in range(width):
                ref[at + x, PAD : PAD + fy, :] = got[(done + x) * fy : (done + x + 1) * fy, :].astype(F32)
        for side, got in zip(y_sides, fld_y):
            at = pl.multiple_of(halo_start(side, cy, 0, PAD + fy), 8)
            block = got[face_rows + f * fx * PAD : face_rows + (f + 1) * fx * PAD, :].astype(F32)
            for x in range(fx):
                ref[WV + x, pl.ds(at, PAD), :] = block[x * PAD : (x + 1) * PAD, :]
        for (x_side, y_side), got in zip(xy_sides, fld_xy):
            at_x = halo_start(x_side, cx, WV - width, WV + fx)
            at = pl.multiple_of(halo_start(y_side, cy, 0, PAD + fy), 8)
            block = got[...].astype(F32)
            for x in range(width):
                ref[at_x + x, pl.ds(at, PAD), :] = block[(done + x) * PAD : (done + x + 1) * PAD, :]

    cells = (bx + 2 * WC) * rc
    wide[...] = exact_dot(coarse[...].reshape(cells, LANES), z_refine(cz))
    for p in range(bx + 2 * WC):
        base, half = p * rc + PAD // 2, ry // 2
        here = 0.75 * wide[pl.ds(base, half), :]
        fine[pl.ds(p * ry, half, stride=2), :] = here + 0.25 * wide[pl.ds(base - 1, half), :]
        fine[pl.ds(p * ry + 1, half, stride=2), :] = here + 0.25 * wide[pl.ds(base + 1, half), :]
    for q in range(1, qx - 1):
        at = q - WV
        here, other = at // 2 + WC, at // 2 + WC + (1 if at % 2 else -1)
        refined = 0.75 * fine[pl.ds(here * ry, ry), :] + 0.25 * fine[pl.ds(other * ry, ry), :]
        src[q] = math.pi * (refined - src[q])

    row = lax.broadcasted_iota(jnp.int32, (ry, LANES), 0) - PAD + fy * cy
    lane = lane_iota(ry) - ZOFF + 2 * BZ * cz
    inside = (row >= 0) & (row < fy * counts[1]) & (lane >= 0) & (lane < 2 * BZ * counts[2])
    share = jnp.where(inside, 1.0 / 6.0, 0.0)
    old, new = v0, v1
    for sweep in range(SWEEPS):
        for q in range(sweep + 1, qx - sweep - 1):
            at = q - WV + fx * cx
            here = old[q]
            total = old[q - 1] + old[q + 1]
            total = total + pltpu.roll(here, 1, 0) + pltpu.roll(here, ry - 1, 0)
            total = total + pltpu.roll(here, 1, 1) + pltpu.roll(here, LANES - 1, 1)
            total = (total + src[q]) * share
            if q < WV or q >= WV + fx:
                total = jnp.where((at >= 0) & (at < fx * counts[0]), total, 0.0)
            new[q] = total
        old, new = new, old

    groups = fy // 4
    lane = lane_iota(groups)
    for x in range(fx):
        r = [old[WV + x, pl.ds(PAD + k, groups, stride=4), :] for k in range(4)]
        r1, r2 = pltpu.roll(r[1], 80, 1), pltpu.roll(r[2], 48, 1)
        potential[pl.ds(3 * groups * x, groups, stride=3), :] = jnp.where(lane < 96, pltpu.roll(r[0], 112, 1), r1)
        potential[pl.ds(3 * groups * x + 1, groups, stride=3), :] = jnp.where(lane < 64, r1, r2)
        potential[pl.ds(3 * groups * x + 2, groups, stride=3), :] = jnp.where(lane < 32, r2, pltpu.roll(r[3], 16, 1))

    send_potential = pltpu.make_async_copy(potential, potential_out, store_potential)
    send_potential.start()

    pieces = []
    for x in range(bx):
        q = WV + 2 * x
        fine[pl.ds(x * ry, ry), :] = 0.125 * (old[q - 1] + old[q + 2]) + 0.375 * (old[q] + old[q + 1])
        rows = [fine[pl.ds(x * ry + PAD + k, BY, stride=2), :] for k in (-1, 0, 1, 2)]
        pieces.append(0.125 * (rows[0] + rows[3]) + 0.375 * (rows[1] + rows[2]))
    back = exact_dot(jnp.concatenate(pieces, 0), z_coarsen())
    rho = (3.0 / math.pi) * pltpu.roll(chip[...], jnp.where(cz == 0, 0, LANES - BZ), 1)
    safe = jnp.where(rho > 0.0, rho, 1.0)
    root = jnp.exp(jnp.log(safe) * (1.0 / 3.0))
    root = root - (root - safe / (root * root)) * (1.0 / 3.0)
    flat[...] = back - jnp.where(rho > 0.0, root, 0.0)

    per = 384 // BZ
    groups = flat.shape[0] // per
    lane = lane_iota(groups)
    r = [pltpu.roll(flat[pl.ds(k, groups, stride=per), :], BZ * k % LANES, 1) for k in range(per)]
    for j in range(3):
        tile = None
        for k in range(per):
            low, high = BZ * k - LANES * j, BZ * (k + 1) - LANES * j
            if high > 0 and low < LANES:
                tile = r[k] if tile is None else jnp.where(lane >= low, r[k], tile)
        wide[pl.ds(j, groups, stride=3), :] = tile
    tiles = BY * BZ // LANES
    for t in range(tiles):
        cut = slice(t * LANES, (t + 1) * LANES)
        effective[:, cut] = wide[pl.ds(t, bx, stride=tiles), :]
    for x in range(bx):
        effective[x : x + 1, :] = effective[x : x + 1, :] + local_potential[x]

    width, half = effective.shape[1], bands // 2
    spread = z_spread(cz)
    lane = lane_iota(half)
    stores = []
    for x in range(bx):
        outer = jnp.dot(zf[x], spread, preferred_element_type=F32)
        low = high = None
        for side, face in zip(y_sides, fld_y):
            halo = -0.5 * face[x * half : (x + 1) * half, :].astype(F32)
            if side != "hi":
                here = jnp.concatenate([halo, pltpu.roll(halo, LANES - BZ, 1)], 0)
                keep = jnp.concatenate([lane, lane], 0) < BZ
                low = jnp.where(keep & (cy > 0), here, 0.0)
            if side != "lo":
                here = jnp.concatenate([pltpu.roll(halo, LANES - BZ, 1), pltpu.roll(halo, LANES - 2 * BZ, 1)], 0)
                keep = jnp.concatenate([lane, lane], 0) >= LANES - BZ
                high = jnp.where(keep & (cy < counts[1] - 1), here, 0.0)
        for t in range(width // LANES):
            cut = slice(t * LANES, (t + 1) * LANES)
            total = inner[x, :, cut] + outer[:, cut] + effective[x : x + 1, cut] * orb[x, :, cut].astype(F32)
            if t == 0:
                total = total + low
            if t == width // LANES - 1:
                total = total + high
            for side, face in zip(x_sides, x_faces):
                if x == 0 and side != "hi":
                    total = total + jnp.where(cx > 0, -0.5, 0.0) * face[:, cut].astype(F32)
                if x == bx - 1 and side != "lo":
                    total = total + jnp.where(cx < counts[0] - 1, -0.5, 0.0) * face[:, cut].astype(F32)
            result[x, :, cut] = total.astype(BF16)
        stores.append(pltpu.make_async_copy(result.at[x], out.at[x], store.at[x]))
        stores[-1].start()
    for copy in stores + [send_potential]:
        copy.wait()


def laplace_kernel(orb, out):
    planes, bands, width = orb.shape
    step = 2 * LANES
    weights = [stencil(step * p % BZ, step) for p in range(3)]
    for j in range(0, width, step):
        columns = min(step, width - j)
        first, last = max(j - LANES, 0), min(j + step + LANES, width)
        skip = first - (j - LANES)
        w = weights[j // step % 3][skip : skip + last - first, :columns]
        here = orb[:, :, first:last].reshape(planes * bands, last - first)
        total = jnp.dot(here, w, preferred_element_type=F32).reshape(planes, bands, columns)
        for x in range(planes):
            near = [orb[n, :, j : j + columns].astype(F32) for n in (x - 1, x + 1) if 0 <= n < planes]
            out[x, :, j : j + columns] = total[x] - 0.5 * sum(near)


def vmem():
    return pl.BlockSpec(memory_space=pltpu.VMEM)


def local(mesh, orbitals, occupations, previous, compensation, local_potential):
    return step(mesh, orbitals, occupations, previous, compensation, local_potential)


def step(mesh, orbitals, occupations, previous, compensation, local_potential):
    domains, groups = mesh.shape["dom"], mesh.shape["band"]
    split_z = 2
    split_y = min(4, domains // 4)
    counts = (domains // (split_y * split_z), split_y, split_z)
    bands, _, bx, width = orbitals.shape
    tiles = width // LANES
    fx, fy = 2 * bx, 2 * BY
    x_sides, y_sides = sides(counts[0]), sides(counts[1])
    xy_sides = [(a, b) for a in x_sides for b in y_sides]
    moves = [{0: s} for s in x_sides] + [{1: s} for s in y_sides] + [{0: a, 1: b} for a, b in xy_sides]
    hbm = pl.BlockSpec(memory_space=pltpu.HBM)

    def shape(*dims, dtype=F32):
        return jax.ShapeDtypeStruct(dims, dtype)

    def params(kib):
        return pltpu.CompilerParams(vmem_limit_bytes=kib * 2**10)

    flat = [a.reshape(fx * fy * 2 * BZ // LANES, LANES) for a in (previous, compensation)]
    mates = [fetch(a, counts, {2: "swap"}) for a in flat]

    orb = jnp.transpose(orbitals.reshape(bands, bx, width), (1, 0, 2))
    part, orb, z_face, *x_faces = pl.pallas_call(
        functools.partial(density_kernel, counts),
        in_specs=[hbm, hbm],
        out_specs=[vmem()] * (3 + len(x_sides)),
        out_shape=[shape(bx * tiles, LANES), shape(*orb.shape, dtype=BF16), shape(bx, bands, LANES, dtype=BF16)]
        + [shape(bands, width, dtype=BF16) for _ in x_sides],
        scratch_shapes=[pltpu.VMEM((1, bands), F32), pltpu.SemaphoreType.DMA((bx,)), pltpu.SemaphoreType.DMA(())],
        compiler_params=params(8 * 1024),
        name="density",
    )(
        pltpu.with_memory_space_constraint(orb, pltpu.HBM),
        pltpu.with_memory_space_constraint(occupations.reshape(1, bands), pltpu.HBM),
    )
    x_faces = [fetch(f, counts, {0: s}) for s, f in zip(x_sides, x_faces)]
    parts = [part]
    for shift in range(1, groups):
        route = [(i, (i + shift) % groups) for i in range(groups)]
        parts.append(lax.ppermute(part, "band", route))
    z_face = fetch(z_face, counts, {2: "swap"})

    inner = pl.pallas_call(
        laplace_kernel,
        in_specs=[vmem()],
        out_specs=vmem(),
        out_shape=shape(bx, bands, width),
        compiler_params=params(16 * 1024),
        cost_estimate=pl.CostEstimate(flops=6 * 10**9, bytes_accessed=8 * 10**6, transcendentals=0),
        name="laplace",
    )(orb)

    rim_rows = [(WV + WS) * fy] * len(x_sides) + [bx * bands // 2 + 2 * fx * PAD] * len(y_sides)
    rim_rows += [(WV + WS + 1) * PAD] * len(xy_sides)
    ext, *rims = pl.pallas_call(
        functools.partial(field_kernel, counts),
        in_specs=[vmem()] * 5,
        out_specs=[vmem()] * (1 + len(rim_rows)),
        out_shape=[shape(2 * fx * fy, LANES)] + [shape(n, LANES, dtype=BF16) for n in rim_rows],
        compiler_params=params(4 * 1024),
        cost_estimate=pl.CostEstimate(flops=3 * 10**9, bytes_accessed=10**6, transcendentals=0),
        name="fields",
    )(orb, *flat, *mates)
    fields = [fetch(r, counts, m) for r, m in zip(rims, moves)]

    rho = pl.pallas_call(
        functools.partial(total_kernel, counts, 1.0 / (bands * groups)),
        in_specs=[vmem()] * groups,
        out_specs=vmem(),
        out_shape=shape(bx * BY, LANES),
        scratch_shapes=[pltpu.VMEM((bx * tiles, LANES), F32)],
        compiler_params=params(1024),
        name="total",
    )(*parts)
    mate = fetch(rho, counts, {2: "swap"})
    cut_rows = [WC * BY] * len(x_sides) + [bx * PAD] * len(y_sides) + [(WC + 1) * PAD] * len(xy_sides)
    chip, *cuts = pl.pallas_call(
        functools.partial(cut_kernel, counts),
        in_specs=[vmem(), vmem()],
        out_specs=[vmem()] * (1 + len(cut_rows)),
        out_shape=[shape(bx * BY, LANES)] + [shape(n, LANES, dtype=BF16) for n in cut_rows],
        compiler_params=params(1024),
        name="cut",
    )(rho, mate)
    densities = [fetch(c, counts, m) for c, m in zip(cuts, moves)]

    rc, ry, qx = BY + 2 * PAD, fy + 2 * PAD, fx + 2 * WV
    local_rows = jnp.transpose(local_potential, (1, 0, 2))
    operands = [chip, ext, local_rows, orb, inner, z_face, *densities, *fields, *x_faces]
    applied, potential = pl.pallas_call(
        functools.partial(finish_kernel, counts),
        in_specs=[vmem()] * len(operands),
        out_specs=[hbm, hbm],
        scratch_shapes=[
            pltpu.VMEM((bx + 2 * WC, rc, LANES), F32),
            pltpu.VMEM(((bx + 2 * WC) * rc, LANES), F32),
            pltpu.VMEM(((bx + 2 * WC) * ry, LANES), F32),
            pltpu.VMEM((qx, ry, LANES), F32),
            pltpu.VMEM((qx, ry, LANES), F32),
            pltpu.VMEM((qx, ry, LANES), F32),
            pltpu.VMEM((bx * BY, LANES), F32),
            pltpu.VMEM((bx, width), F32),
            pltpu.VMEM(flat[0].shape, F32),
            pltpu.VMEM((bx, bands, width), BF16),
            pltpu.SemaphoreType.DMA((bx,)),
            pltpu.SemaphoreType.DMA(()),
        ],
        out_shape=[shape(bx, bands, width, dtype=BF16), shape(*flat[0].shape)],
        compiler_params=params(20 * 1024),
        name="finish",
    )(*operands)
    applied = jnp.transpose(applied, (1, 0, 2)).reshape(orbitals.shape)
    return applied, potential.reshape(previous.shape)


def solution(mesh):
    return jax.shard_map(
        functools.partial(local, mesh),
        mesh=mesh,
        in_specs=(
            P("band", "dom", None, None),
            P("band"),
            P("dom", None, None),
            P("dom", None, None),
            P("dom", None, None),
        ),
        out_specs=(P("band", "dom", None, None), P("dom", None, None)),
        check_vma=False,
    )
```

profile of v0, /device:TPU:0, one launch (start us, length us, event | category | flops | bytes accessed | tf_op | source)
XLA Modules:
  0.0 40.6 jit_solution(5990434040411830827)
XLA Ops:
  0.6 0.0 copy-start.1
  0.6 0.0 copy-start.2
  0.7 0.6 %collective-permute-start.4 = (f32[432,128]{1,0:T(8,128)}, f32[432,128]{1,0:T(8,128)S(1)}, u32[]{:S(2)}, u32[]{:S(2)}) collective-permute-start(f32[432,128]{1,0:T(8,128)} %bitcast.12), channel_id=1, source_target_pairs={{4,0},{0,4},{12,8},{8,12},{20,16},{16,20},{28,24},{24,28},{5,1},{1... | collective-permute-start | bytes 663560 | tf_op jit(solution)/shard_map/ppermute | solution.py:38
  1.2 0.1 collective-permute-start.5
  1.3 3.4 %density.1 = (f32[54,128]{1,0:T(8,128)S(1)}, bf16[6,192,1152]{2,1,0:T(8,128)(2,1)S(1)}, bf16[6,192,128]{2,1,0:T(8,128)(2,1)S(1)}, bf16[192,1152]{1,0:T(8,128)(2,1)S(1)}) custom-call(bf16[6,192,1152]{2,1,0:T(8,128)(2,1)} %bitcast.16, f32[1,192]{1,0:T(1,128)} %bitcast.17), custom_call_target="tpu_custom_call" | custom-call | tf_op jit(solution)/shard_map/density/pallas_call | solution.py:469
  4.7 5.1 %collective-permute-start.2 = (f32[54,128]{1,0:T(8,128)S(1)}, f32[54,128]{1,0:T(8,128)S(1)}, u32[]{:S(2)}, u32[]{:S(2)}) collective-permute-start(f32[54,128]{1,0:T(8,128)S(1)} %get-tuple-element.16.refs_0_), channel_id=1, source_target_pairs={{0,3},{1,0},{2,1},{3,2},{4,7},{5,4},{6,5},{7,6},{8,11},{9,8},{10,9... | collective-permute-start | bytes 82952 | tf_op jit(solution)/shard_map/ppermute | solution.py:486
  9.8 0.0 collective-permute-start.1
  9.8 1.0 %collective-permute-start = (f32[54,128]{1,0:T(8,128)S(1)}, f32[54,128]{1,0:T(8,128)S(1)}, u32[]{:S(2)}, u32[]{:S(2)}) collective-permute-start(f32[54,128]{1,0:T(8,128)S(1)} %get-tuple-element.16.refs_0_), channel_id=1, source_target_pairs={{0,1},{1,2},{2,3},{3,0},{4,5},{5,6},{6,7},{7,4},{8,9},{9,10},{10,1... | collective-permute-start | bytes 82952 | tf_op jit(solution)/shard_map/ppermute | solution.py:486
  10.8 0.6 %collective-permute-done.2.refs_3_ = f32[54,128]{1,0:T(8,128)S(1)} collective-permute-done((f32[54,128]{1,0:T(8,128)S(1)}, f32[54,128]{1,0:T(8,128)S(1)}, u32[]{:S(2)}, u32[]{:S(2)}) %collective-permute-start.2) | collective-permute-done | bytes 27680 | tf_op jit(solution)/shard_map/ppermute | solution.py:486
  11.3 3.2 %collective-permute-done.1.refs_2_ = f32[54,128]{1,0:T(8,128)S(1)} collective-permute-done((f32[54,128]{1,0:T(8,128)S(1)}, f32[54,128]{1,0:T(8,128)S(1)}, u32[]{:S(2)}, u32[]{:S(2)}) %collective-permute-start.1) | collective-permute-done | bytes 27680 | tf_op jit(solution)/shard_map/ppermute | solution.py:486
  14.6 0.9 %collective-permute-done.refs_1_ = f32[54,128]{1,0:T(8,128)S(1)} collective-permute-done((f32[54,128]{1,0:T(8,128)S(1)}, f32[54,128]{1,0:T(8,128)S(1)}, u32[]{:S(2)}, u32[]{:S(2)}) %collective-permute-start) | collective-permute-done | bytes 27680 | tf_op jit(solution)/shard_map/ppermute | solution.py:486
  15.4 0.2 total.1.rho
  15.6 0.1 collective-permute-start.3
  15.7 0.5 %collective-permute-start.6 = (bf16[6,192,128]{2,1,0:T(8,128)(2,1)S(1)}, bf16[6,192,128]{2,1,0:T(8,128)(2,1)S(1)}, u32[]{:S(2)}, u32[]{:S(2)}) collective-permute-start(bf16[6,192,128]{2,1,0:T(8,128)(2,1)S(1)} %get-tuple-element.20), channel_id=1, source_target_pairs={{4,0},{0,4},{12,8},{8,12},{20,16},{16,20},{28,24},{24,28},{5,1},{1... | collective-permute-start | bytes 884744 | tf_op jit(solution)/shard_map/ppermute | solution.py:38
  16.2 1.5 %collective-permute-start.13 = (bf16[192,1152]{1,0:T(8,128)(2,1)S(1)}, bf16[192,1152]{1,0:T(8,128)(2,1)S(1)}, u32[]{:S(2)}, u32[]{:S(2)}) collective-permute-start(bf16[192,1152]{1,0:T(8,128)(2,1)S(1)} %get-tuple-element.27), channel_id=1, source_target_pairs={{16,0},{20,4},{24,8},{28,12},{0,16},{4,20},{8,24},{12,28},{17,1},{... | collective-permute-start | bytes 1327112 | tf_op jit(solution)/shard_map/ppermute | solution.py:38
  17.7 0.0 collective-permute-done.3.mate
  17.8 1.7 %collective-permute-start.9 = (bf16[32,128]{1,0:T(8,128)(2,1)S(1)}, bf16[32,128]{1,0:T(8,128)(2,1)S(1)}, u32[]{:S(2)}, u32[]{:S(2)}) collective-permute-start(bf16[32,128]{1,0:T(8,128)(2,1)S(1)} %get-tuple-element.23), channel_id=1, source_target_pairs={{24,0},{28,4},{16,8},{20,12},{8,16},{12,20},{0,24},{4,28},{25,1},{... | collective-permute-start | bytes 24584 | tf_op jit(solution)/shard_map/ppermute | solution.py:38
  19.5 0.0 collective-permute-done.4.mate_prev
  19.5 0.5 %collective-permute-start.8 = (bf16[48,128]{1,0:T(8,128)(2,1)S(1)}, bf16[48,128]{1,0:T(8,128)(2,1)S(1)}, u32[]{:S(2)}, u32[]{:S(2)}) collective-permute-start(bf16[48,128]{1,0:T(8,128)(2,1)S(1)} %get-tuple-element.22), channel_id=1, source_target_pairs={{8,0},{12,4},{0,8},{4,12},{24,16},{28,20},{16,24},{20,28},{9,1},{1... | collective-permute-start | bytes 36872 | tf_op jit(solution)/shard_map/ppermute | solution.py:38
  20.0 0.0 collective-permute-done.5.mate_comp
  20.0 1.3 %collective-permute-start.7 = (bf16[72,128]{1,0:T(8,128)(2,1)S(1)}, bf16[72,128]{1,0:T(8,128)(2,1)S(1)}, u32[]{:S(2)}, u32[]{:S(2)}) collective-permute-start(bf16[72,128]{1,0:T(8,128)(2,1)S(1)} %get-tuple-element.21), channel_id=1, source_target_pairs={{16,0},{20,4},{24,8},{28,12},{0,16},{4,20},{8,24},{12,28},{17,1},{... | collective-permute-start | bytes 55304 | tf_op jit(solution)/shard_map/ppermute | solution.py:38
  21.3 0.0 copy-done.1
  21.3 0.0 copy-done.2
  21.3 0.8 %fields.1 = (f32[1152,128]{1,0:T(8,128)S(1)}, bf16[432,128]{1,0:T(8,128)(2,1)S(1)}, bf16[768,128]{1,0:T(8,128)(2,1)S(1)}, bf16[80,128]{1,0:T(8,128)(2,1)S(1)}) custom-call(bf16[6,192,1152]{2,1,0:T(8,128)(2,1)S(1)} %get-tuple-element.18.orb.refs_3_, f32[432,128]{1,0:T(8,128)S(1)} %bitcast.13, f32[432,128]{1,0:T(8,128)S(1)} %bitcast.15, ...), custom_call_target="tpu_custom_call" | custom-call | flops 3000000000 | bytes 1000000 | tf_op jit(solution)/shard_map/fields/pallas_call | solution.py:501
  22.1 0.4 collective-permute-done.9.refs_8_
  22.5 1.7 %collective-permute-start.12 = (bf16[80,128]{1,0:T(8,128)(2,1)S(1)}, bf16[80,128]{1,0:T(8,128)(2,1)S(1)}, u32[]{:S(2)}, u32[]{:S(2)}) collective-permute-start(bf16[80,128]{1,0:T(8,128)(2,1)S(1)} %get-tuple-element.26), channel_id=1, source_target_pairs={{24,0},{28,4},{16,8},{20,12},{8,16},{12,20},{0,24},{4,28},{25,1},{... | collective-permute-start | bytes 61448 | tf_op jit(solution)/shard_map/ppermute | solution.py:38
  24.1 0.0 collective-permute-done.8.refs_7_
  24.2 1.3 %collective-permute-start.10 = (bf16[432,128]{1,0:T(8,128)(2,1)S(1)}, bf16[432,128]{1,0:T(8,128)(2,1)S(1)}, u32[]{:S(2)}, u32[]{:S(2)}) collective-permute-start(bf16[432,128]{1,0:T(8,128)(2,1)S(1)} %get-tuple-element.24), channel_id=1, source_target_pairs={{16,0},{20,4},{24,8},{28,12},{0,16},{4,20},{8,24},{12,28},{17,1},{... | collective-permute-start | bytes 331784 | tf_op jit(solution)/shard_map/ppermute | solution.py:38
  25.4 4.8 %collective-permute-done.7.refs_6_ = bf16[72,128]{1,0:T(8,128)(2,1)S(1)} collective-permute-done((bf16[72,128]{1,0:T(8,128)(2,1)S(1)}, bf16[72,128]{1,0:T(8,128)(2,1)S(1)}, u32[]{:S(2)}, u32[]{:S(2)}) %collective-permute-start.7) | collective-permute-done | bytes 18464 | tf_op jit(solution)/shard_map/ppermute | solution.py:38
  30.3 0.0 copy-start
  30.3 1.5 %collective-permute-start.11 = (bf16[768,128]{1,0:T(8,128)(2,1)S(1)}, bf16[768,128]{1,0:T(8,128)(2,1)S(1)}, u32[]{:S(2)}, u32[]{:S(2)}) collective-permute-start(bf16[768,128]{1,0:T(8,128)(2,1)S(1)} %get-tuple-element.25), channel_id=1, source_target_pairs={{8,0},{12,4},{0,8},{4,12},{24,16},{28,20},{16,24},{20,28},{9,1},{1... | collective-permute-start | bytes 589832 | tf_op jit(solution)/shard_map/ppermute | solution.py:38
  31.7 1.7 %laplace.1.refs_4_ = f32[6,192,1152]{2,1,0:T(8,128)S(1)} custom-call(bf16[6,192,1152]{2,1,0:T(8,128)(2,1)S(1)} %get-tuple-element.18.orb.refs_3_), custom_call_target="tpu_custom_call" | custom-call | flops 6000000000 | bytes 8000000 | tf_op jit(solution)/shard_map/laplace/pallas_call | solution.py:489
  33.4 0.0 collective-permute-done.12.refs_11_
  33.4 0.0 collective-permute-done.6.refs_5_
  33.4 0.0 collective-permute-done.10.refs_9_
  33.4 2.5 %collective-permute-done.11.refs_10_ = bf16[768,128]{1,0:T(8,128)(2,1)S(1)} collective-permute-done((bf16[768,128]{1,0:T(8,128)(2,1)S(1)}, bf16[768,128]{1,0:T(8,128)(2,1)S(1)}, u32[]{:S(2)}, u32[]{:S(2)}) %collective-permute-start.11) | collective-permute-done | bytes 196640 | tf_op jit(solution)/shard_map/ppermute | solution.py:38
  35.9 0.0 collective-permute-done.13.refs_12_
  35.9 0.0 copy-done
  35.9 4.6 %finish.1 = (bf16[6,192,1152]{2,1,0:T(8,128)(2,1)}, f32[432,128]{1,0:T(8,128)}) custom-call(f32[144,128]{1,0:T(8,128)S(1)} %get-tuple-element.17.refs_0_, f32[1152,128]{1,0:T(8,128)S(1)} %get-tuple-element.19.refs_1_, f32[6,1,1152]{2,1,0:T(1,128)S(1)} %bitcast.11, bf16[6,192,1152]{2,1,0:T(8,128)(2,1)S(1)} %get-tuple-element.18.orb.refs_3_, ...), custom_call_target="tpu_custom_call" | custom-call | tf_op jit(solution)/shard_map/finish/pallas_call | solution.py:536
  (1 shorter events, 0.0 us)
Async XLA Ops:
  0.6 20.7 %copy-start.1 = (f32[1,12,4608]{2,0,1:T(1,128)S(1)}, f32[1,12,4608]{2,0,1:T(1,128)}, u32[]{:S(2)}) copy-start(f32[1,12,4608]{2,0,1:T(1,128)} %param.7) | copy-start | bytes 663556
  0.6 20.7 %copy-start.2 = (f32[1,12,4608]{2,0,1:T(1,128)S(1)}, f32[1,12,4608]{2,0,1:T(1,128)}, u32[]{:S(2)}) copy-start(f32[1,12,4608]{2,0,1:T(1,128)} %param.8) | copy-start | bytes 663556
  0.7 18.9 %collective-permute-start.4 = (f32[432,128]{1,0:T(8,128)}, f32[432,128]{1,0:T(8,128)S(1)}, u32[]{:S(2)}, u32[]{:S(2)}) collective-permute-start(f32[432,128]{1,0:T(8,128)} %bitcast.12), channel_id=1, source_target_pairs={{4,0},{0,4},{12,8},{8,12},{20,16},{16,20},{28,24},{24,28},{5,1},{1... | collective-permute-start | bytes 663560 | tf_op jit(solution)/shard_map/ppermute | solution.py:38
  1.2 18.8 %collective-permute-start.5 = (f32[432,128]{1,0:T(8,128)}, f32[432,128]{1,0:T(8,128)S(1)}, u32[]{:S(2)}, u32[]{:S(2)}) collective-permute-start(f32[432,128]{1,0:T(8,128)} %bitcast.14), channel_id=1, source_target_pairs={{4,0},{0,4},{12,8},{8,12},{20,16},{16,20},{28,24},{24,28},{5,1},{1... | collective-permute-start | bytes 663560 | tf_op jit(solution)/shard_map/ppermute | solution.py:38
  4.7 6.6 %collective-permute-start.2 = (f32[54,128]{1,0:T(8,128)S(1)}, f32[54,128]{1,0:T(8,128)S(1)}, u32[]{:S(2)}, u32[]{:S(2)}) collective-permute-start(f32[54,128]{1,0:T(8,128)S(1)} %get-tuple-element.16.refs_0_), channel_id=1, source_target_pairs={{0,3},{1,0},{2,1},{3,2},{4,7},{5,4},{6,5},{7,6},{8,11},{9,8},{10,9... | collective-permute-start | bytes 82952 | tf_op jit(solution)/shard_map/ppermute | solution.py:486
  9.8 4.8 %collective-permute-start.1 = (f32[54,128]{1,0:T(8,128)S(1)}, f32[54,128]{1,0:T(8,128)S(1)}, u32[]{:S(2)}, u32[]{:S(2)}) collective-permute-start(f32[54,128]{1,0:T(8,128)S(1)} %get-tuple-element.16.refs_0_), channel_id=1, source_target_pairs={{0,2},{1,3},{2,0},{3,1},{4,6},{5,7},{6,4},{7,5},{8,10},{9,11},{10,... | collective-permute-start | bytes 82952 | tf_op jit(solution)/shard_map/ppermute | solution.py:486
  9.8 5.7 %collective-permute-start = (f32[54,128]{1,0:T(8,128)S(1)}, f32[54,128]{1,0:T(8,128)S(1)}, u32[]{:S(2)}, u32[]{:S(2)}) collective-permute-start(f32[54,128]{1,0:T(8,128)S(1)} %get-tuple-element.16.refs_0_), channel_id=1, source_target_pairs={{0,1},{1,2},{2,3},{3,0},{4,5},{5,6},{6,7},{7,4},{8,9},{9,10},{10,1... | collective-permute-start | bytes 82952 | tf_op jit(solution)/shard_map/ppermute | solution.py:486
  15.6 2.1 %collective-permute-start.3 = (f32[144,128]{1,0:T(8,128)S(1)}, f32[144,128]{1,0:T(8,128)S(1)}, u32[]{:S(2)}, u32[]{:S(2)}) collective-permute-start(f32[144,128]{1,0:T(8,128)S(1)} %total.1.rho), channel_id=1, source_target_pairs={{4,0},{0,4},{12,8},{8,12},{20,16},{16,20},{28,24},{24,28},{5,1},{1... | collective-permute-start | bytes 221192 | tf_op jit(solution)/shard_map/ppermute | solution.py:38
  15.7 17.7 %collective-permute-start.6 = (bf16[6,192,128]{2,1,0:T(8,128)(2,1)S(1)}, bf16[6,192,128]{2,1,0:T(8,128)(2,1)S(1)}, u32[]{:S(2)}, u32[]{:S(2)}) collective-permute-start(bf16[6,192,128]{2,1,0:T(8,128)(2,1)S(1)} %get-tuple-element.20), channel_id=1, source_target_pairs={{4,0},{0,4},{12,8},{8,12},{20,16},{16,20},{28,24},{24,28},{5,1},{1... | collective-permute-start | bytes 884744 | tf_op jit(solution)/shard_map/ppermute | solution.py:38
  16.2 19.7 %collective-permute-start.13 = (bf16[192,1152]{1,0:T(8,128)(2,1)S(1)}, bf16[192,1152]{1,0:T(8,128)(2,1)S(1)}, u32[]{:S(2)}, u32[]{:S(2)}) collective-permute-start(bf16[192,1152]{1,0:T(8,128)(2,1)S(1)} %get-tuple-element.27), channel_id=1, source_target_pairs={{16,0},{20,4},{24,8},{28,12},{0,16},{4,20},{8,24},{12,28},{17,1},{... | collective-permute-start | bytes 1327112 | tf_op jit(solution)/shard_map/ppermute | solution.py:38
  17.8 4.7 %collective-permute-start.9 = (bf16[32,128]{1,0:T(8,128)(2,1)S(1)}, bf16[32,128]{1,0:T(8,128)(2,1)S(1)}, u32[]{:S(2)}, u32[]{:S(2)}) collective-permute-start(bf16[32,128]{1,0:T(8,128)(2,1)S(1)} %get-tuple-element.23), channel_id=1, source_target_pairs={{24,0},{28,4},{16,8},{20,12},{8,16},{12,20},{0,24},{4,28},{25,1},{... | collective-permute-start | bytes 24584 | tf_op jit(solution)/shard_map/ppermute | solution.py:38
  19.5 4.7 %collective-permute-start.8 = (bf16[48,128]{1,0:T(8,128)(2,1)S(1)}, bf16[48,128]{1,0:T(8,128)(2,1)S(1)}, u32[]{:S(2)}, u32[]{:S(2)}) collective-permute-start(bf16[48,128]{1,0:T(8,128)(2,1)S(1)} %get-tuple-element.22), channel_id=1, source_target_pairs={{8,0},{12,4},{0,8},{4,12},{24,16},{28,20},{16,24},{20,28},{9,1},{1... | collective-permute-start | bytes 36872 | tf_op jit(solution)/shard_map/ppermute | solution.py:38
  20.0 10.2 %collective-permute-start.7 = (bf16[72,128]{1,0:T(8,128)(2,1)S(1)}, bf16[72,128]{1,0:T(8,128)(2,1)S(1)}, u32[]{:S(2)}, u32[]{:S(2)}) collective-permute-start(bf16[72,128]{1,0:T(8,128)(2,1)S(1)} %get-tuple-element.21), channel_id=1, source_target_pairs={{16,0},{20,4},{24,8},{28,12},{0,16},{4,20},{8,24},{12,28},{17,1},{... | collective-permute-start | bytes 55304 | tf_op jit(solution)/shard_map/ppermute | solution.py:38
  22.5 10.9 %collective-permute-start.12 = (bf16[80,128]{1,0:T(8,128)(2,1)S(1)}, bf16[80,128]{1,0:T(8,128)(2,1)S(1)}, u32[]{:S(2)}, u32[]{:S(2)}) collective-permute-start(bf16[80,128]{1,0:T(8,128)(2,1)S(1)} %get-tuple-element.26), channel_id=1, source_target_pairs={{24,0},{28,4},{16,8},{20,12},{8,16},{12,20},{0,24},{4,28},{25,1},{... | collective-permute-start | bytes 61448 | tf_op jit(solution)/shard_map/ppermute | solution.py:38
  24.2 9.3 %collective-permute-start.10 = (bf16[432,128]{1,0:T(8,128)(2,1)S(1)}, bf16[432,128]{1,0:T(8,128)(2,1)S(1)}, u32[]{:S(2)}, u32[]{:S(2)}) collective-permute-start(bf16[432,128]{1,0:T(8,128)(2,1)S(1)} %get-tuple-element.24), channel_id=1, source_target_pairs={{16,0},{20,4},{24,8},{28,12},{0,16},{4,20},{8,24},{12,28},{17,1},{... | collective-permute-start | bytes 331784 | tf_op jit(solution)/shard_map/ppermute | solution.py:38
  30.3 5.7 %copy-start = (f32[1,6,1152]{2,0,1:T(1,128)S(1)}, f32[1,6,1152]{2,0,1:T(1,128)}, u32[]{:S(2)}) copy-start(f32[1,6,1152]{2,0,1:T(1,128)} %param.9) | copy-start | bytes 82948
  30.3 5.7 %collective-permute-start.11 = (bf16[768,128]{1,0:T(8,128)(2,1)S(1)}, bf16[768,128]{1,0:T(8,128)(2,1)S(1)}, u32[]{:S(2)}, u32[]{:S(2)}) collective-permute-start(bf16[768,128]{1,0:T(8,128)(2,1)S(1)} %get-tuple-element.25), channel_id=1, source_target_pairs={{8,0},{12,4},{0,8},{4,12},{24,16},{28,20},{16,24},{20,28},{9,1},{1... | collective-permute-start | bytes 589832 | tf_op jit(solution)/shard_map/ppermute | solution.py:38
where the time goes:
time: 40.7 us; the launch traced here: 40.6 us
  starting transfers between devices  16.8 us (41%)
  waiting for transfers between devices  12.4 us (30%)
  Pallas kernels  10.7 us (26%)
  between operations  0.72 us (2%)
    ppermute x11, starting transfers between devices, fetch(): return lax.ppermute(block, 'dom', pairs)  10.7 us
    ppermute x11, waiting for transfers between devices, fetch(): return lax.ppermute(block, 'dom', pairs)  7.71 us
    ppermute x3, starting transfers between devices, step(): parts.append(lax.ppermute(part, 'band', route))  6.08 us
    ppermute x3, waiting for transfers between devices, step(): parts.append(lax.ppermute(part, 'band', route))  4.66 us
    pallas_call x1, Pallas kernels, step(): pl.pallas_call(functools.partial(finish_kernel, counts), in_specs=[vmem()...  4.62 us
    pallas_call x1, Pallas kernels, step(): pl.pallas_call(functools.partial(density_kernel, counts), in_specs=[hbm,...  3.41 us
    pallas_call x1, Pallas kernels, step(): pl.pallas_call(laplace_kernel, in_specs=[vmem()], out_specs=vmem(), out_s...  1.66 us
  transfers between devices with their start and end apart: 14, of which 6 were waited for; matrix products, arithmetic and copies ran while one was open for 0% of the time, Pallas kernels for 15%

commit v1 on v0

--- a/solution.py
+++ b/solution.py
@@ -59,13 +59,13 @@
     return lax.broadcasted_iota(jnp.int32, (rows, LANES), 1)
 
 
-def exact_dot(value, weights):
+def halves(value):
     high = value.astype(BF16)
-    rest = value - high.astype(F32)
-    middle = rest.astype(BF16)
-    low = (rest - middle.astype(F32)).astype(BF16)
-    dot = functools.partial(jnp.dot, preferred_element_type=F32)
-    return dot(high, weights) + (dot(middle, weights) + dot(low, weights))
+    return jnp.concatenate([high, (value - high.astype(F32)).astype(BF16)], 1)
+
+
+def wide_dot(value, weights):
+    return jnp.dot(halves(value), jnp.concatenate([weights, weights], 0), preferred_element_type=F32)
 
 
 def grid2(rows, columns):
@@ -88,14 +88,24 @@
     return jnp.where(cell < BZ, w, 0.0).astype(BF16)
 
 
-def z_pick(core):
-    lane, y = grid2(BY * BZ, LANES)
+def z_neighbours():
+    source, lane = grid2(LANES, LANES)
+    step = source - lane
+    return jnp.where((step == 1) | (step == -1), 1.0, 0.0).astype(BF16)
+
+
+def z_pick(core, lanes):
+    lane, y = grid2(lanes, LANES)
     return jnp.where(lane == BZ * y + jnp.where(core == 0, BZ - 1, 0), 1.0, 0.0).astype(BF16)
 
 
 def z_spread(core):
     y, lane = grid2(LANES, BY * BZ)
     return jnp.where(lane == BZ * y + jnp.where(core == 0, BZ - 1, 0), -0.5, 0.0).astype(BF16)
+
+
+def lanes_of(value, index):
+    return jnp.take_along_axis(value, index, axis=1, mode="promise_in_bounds")
 
 
 def stencil(first, columns):
@@ -125,17 +135,23 @@
     loads = [pltpu.make_async_copy(orb.at[x], held.at[x], load.at[x]) for x in range(planes)]
     for copy in loads:
         copy.start()
-    pick = z_pick(pos[2])
+    split = min(4, tiles)
+    pick = z_pick(pos[2], split * LANES)
+    face_lane = lane_iota(bands) * BZ + jnp.where(pos[2] == 0, BZ - 1, 0)
     first.wait()
     rows = jnp.broadcast_to(weights[...], (LANES, bands))
     rows = jnp.concatenate([rows, jnp.zeros((LANES, -bands % LANES), F32)], 1)
     weight = jnp.concatenate([rows[:, b : b + LANES].T for b in range(0, bands, LANES)], 0)[:bands]
     for x in range(planes):
         loads[x].wait()
+        face = jnp.dot(held[x, :, : split * LANES], pick, preferred_element_type=F32)
         for t in range(tiles):
             f = held[x, :, t * LANES : (t + 1) * LANES].astype(F32)
             part[tiles * x + t : tiles * x + t + 1, :] = sum_rows(f * f * weight)
-        zf[x] = jnp.dot(held[x], pick, preferred_element_type=F32).astype(BF16)
+            if t >= split:
+                at = face_lane - t * LANES
+                face = jnp.where(at >= 0, lanes_of(f, at & (LANES - 1)), face)
+        zf[x] = face.astype(BF16)
     for side, face in zip(sides(counts[0]), x_faces):
         face[...] = held[rim_start(side, pos[0], planes, 1)]
 
@@ -160,11 +176,12 @@
         out[pl.ds(k, groups, stride=per), :] = pltpu.roll(row, shift, 1)
 
 
-def cut_kernel(counts, rho, mate, chip, *sends):
+def cut_kernel(counts, rho, mate, *refs):
+    x_sides, y_sides = sides(counts[0]), sides(counts[1])
+    corners = len(x_sides) * len(y_sides)
+    fields, chip, sends = list(refs[:corners]), refs[corners], list(refs[corners + 1 :])
     cx, cy, _ = position(counts)
     chip[...] = rho[...] + mate[...]
-    sends = list(sends)
-    x_sides, y_sides = sides(counts[0]), sides(counts[1])
     bx = chip.shape[0] // BY
     for side in x_sides:
         at = pl.multiple_of(BY * rim_start(side, cx, bx, WC), 8)
@@ -178,7 +195,8 @@
             at_x, at = rim_start(x_side, cx, bx, WC), rim_start(y_side, cy, BY, PAD)
             rows = [chip[pl.ds(pl.multiple_of(BY * (at_x + x) + at, 8), PAD), :] for x in range(WC)]
             rows.append(jnp.zeros((PAD, LANES), F32))
-            sends.pop(0)[...] = jnp.concatenate(rows, 0).astype(BF16)
+            rows = jnp.concatenate(rows, 0).astype(BF16)
+            sends.pop(0)[...] = jnp.concatenate([rows, fields.pop(0)[...]], 0)
 
 
 def field_rows(ref, groups):
@@ -248,13 +266,43 @@
             send[...] = jnp.concatenate(cut, 0).astype(BF16)
 
 
+def merge_rows(flat, joined):
+    per = 384 // BZ
+    groups = flat.shape[0] // per
+    lane = lane_iota(groups)
+    r = [pltpu.roll(flat[pl.ds(k, groups, stride=per), :], BZ * k % LANES, 1) for k in range(per)]
+    for j in range(3):
+        tile = None
+        for k in range(per):
+            low, high = BZ * k - LANES * j, BZ * (k + 1) - LANES * j
+            if high > 0 and low < LANES:
+                tile = r[k] if tile is None else jnp.where(lane >= low, r[k], tile)
+        joined[pl.ds(j, groups, stride=3), :] = tile
+    tiles = BY * BZ // LANES
+    planes = flat.shape[0] // BY
+    columns = [joined[pl.ds(t, planes, stride=tiles), :] for t in range(tiles)]
+    rows = jnp.concatenate(columns, 1)
+    return [rows[x : x + 1] for x in range(planes)]
+
+
+def local_kernel(counts, chip, local_potential, out, flat, joined):
+    cz = position(counts)[2]
+    rho = (3.0 / math.pi) * pltpu.roll(chip[...], jnp.where(cz == 0, 0, LANES - BZ), 1)
+    safe = jnp.where(rho > 0.0, rho, 1.0)
+    root = jnp.exp(jnp.log(safe) * (1.0 / 3.0))
+    root = root - (root - safe / (root * root)) * (1.0 / 3.0)
+    flat[...] = jnp.where(rho > 0.0, root, 0.0)
+    for x, row in enumerate(merge_rows(flat, joined)):
+        out[x : x + 1, :] = local_potential[x] - row
+
+
 def finish_kernel(counts, *refs):
     it = iter(refs)
-    chip, ext, local_potential, orb, inner, zf = (next(it) for _ in range(6))
+    chip, ext, local_part, orb, inner, zf = (next(it) for _ in range(6))
     x_sides, y_sides = sides(counts[0]), sides(counts[1])
     xy_sides = [(a, b) for a in x_sides for b in y_sides]
     rho_x, rho_y, rho_xy = ([next(it) for _ in s] for s in (x_sides, y_sides, xy_sides))
-    fld_x, fld_y, fld_xy = ([next(it) for _ in s] for s in (x_sides, y_sides, xy_sides))
+    fld_x, fld_y = ([next(it) for _ in s] for s in (x_sides, y_sides))
     x_faces = [next(it) for _ in x_sides]
     out, potential_out = next(it), next(it)
     coarse, wide, fine, v0, v1, src, flat, effective, potential, result, store, store_potential = it
@@ -287,6 +335,8 @@
             coarse[at_x + x, pl.ds(at, PAD), :] = block[x * PAD : (x + 1) * PAD, :]
 
     v0[...] = jnp.zeros_like(v0)
+    v1[:, 0:PAD, :] = jnp.zeros((qx, PAD, LANES), F32)
+    v1[:, ry - PAD : ry, :] = jnp.zeros((qx, PAD, LANES), F32)
     src[...] = jnp.zeros_like(src)
     for f, (ref, width) in enumerate(((v0, WV), (src, WS))):
         rows = f * fx * fy
@@ -302,15 +352,15 @@
             block = got[face_rows + f * fx * PAD : face_rows + (f + 1) * fx * PAD, :].astype(F32)
             for x in range(fx):
                 ref[WV + x, pl.ds(at, PAD), :] = block[x * PAD : (x + 1) * PAD, :]
-        for (x_side, y_side), got in zip(xy_sides, fld_xy):
+        for (x_side, y_side), got in zip(xy_sides, rho_xy):
             at_x = halo_start(x_side, cx, WV - width, WV + fx)
             at = pl.multiple_of(halo_start(y_side, cy, 0, PAD + fy), 8)
-            block = got[...].astype(F32)
+            block = got[(WC + 1) * PAD :, :].astype(F32)
             for x in range(width):
                 ref[at_x + x, pl.ds(at, PAD), :] = block[(done + x) * PAD : (done + x + 1) * PAD, :]
 
     cells = (bx + 2 * WC) * rc
-    wide[...] = exact_dot(coarse[...].reshape(cells, LANES), z_refine(cz))
+    wide[...] = wide_dot(coarse[...].reshape(cells, LANES), z_refine(cz))
     for p in range(bx + 2 * WC):
         base, half = p * rc + PAD // 2, ry // 2
         here = 0.75 * wide[pl.ds(base, half), :]
@@ -322,22 +372,26 @@
         refined = 0.75 * fine[pl.ds(here * ry, ry), :] + 0.25 * fine[pl.ds(other * ry, ry), :]
         src[q] = math.pi * (refined - src[q])
 
-    row = lax.broadcasted_iota(jnp.int32, (ry, LANES), 0) - PAD + fy * cy
-    lane = lane_iota(ry) - ZOFF + 2 * BZ * cz
+    near, span = PAD - WS, fy + 2 * WS
+    row = lax.broadcasted_iota(jnp.int32, (span, LANES), 0) - WS + fy * cy
+    lane = lane_iota(span) - ZOFF + 2 * BZ * cz
     inside = (row >= 0) & (row < fy * counts[1]) & (lane >= 0) & (lane < 2 * BZ * counts[2])
     share = jnp.where(inside, 1.0 / 6.0, 0.0)
     old, new = v0, v1
+    beside = z_neighbours()
     for sweep in range(SWEEPS):
-        for q in range(sweep + 1, qx - sweep - 1):
+        first, last = sweep + 1, qx - sweep - 1
+        rows = old[first:last, near : near + span, :].reshape((last - first) * span, LANES)
+        along_z = wide_dot(rows, beside)
+        for q in range(first, last):
             at = q - WV + fx * cx
-            here = old[q]
-            total = old[q - 1] + old[q + 1]
-            total = total + pltpu.roll(here, 1, 0) + pltpu.roll(here, ry - 1, 0)
-            total = total + pltpu.roll(here, 1, 1) + pltpu.roll(here, LANES - 1, 1)
-            total = (total + src[q]) * share
+            total = along_z[(q - first) * span : (q - first + 1) * span]
+            total = total + old[q - 1, near : near + span, :] + old[q + 1, near : near + span, :]
+            total = total + old[q, near - 1 : near - 1 + span, :] + old[q, near + 1 : near + 1 + span, :]
+            total = (total + src[q, near : near + span, :]) * share
             if q < WV or q >= WV + fx:
                 total = jnp.where((at >= 0) & (at < fx * counts[0]), total, 0.0)
-            new[q] = total
+            new[q, near : near + span, :] = total
         old, new = new, old
 
     groups = fy // 4
@@ -358,62 +412,43 @@
         fine[pl.ds(x * ry, ry), :] = 0.125 * (old[q - 1] + old[q + 2]) + 0.375 * (old[q] + old[q + 1])
         rows = [fine[pl.ds(x * ry + PAD + k, BY, stride=2), :] for k in (-1, 0, 1, 2)]
         pieces.append(0.125 * (rows[0] + rows[3]) + 0.375 * (rows[1] + rows[2]))
-    back = exact_dot(jnp.concatenate(pieces, 0), z_coarsen())
-    rho = (3.0 / math.pi) * pltpu.roll(chip[...], jnp.where(cz == 0, 0, LANES - BZ), 1)
-    safe = jnp.where(rho > 0.0, rho, 1.0)
-    root = jnp.exp(jnp.log(safe) * (1.0 / 3.0))
-    root = root - (root - safe / (root * root)) * (1.0 / 3.0)
-    flat[...] = back - jnp.where(rho > 0.0, root, 0.0)
-
-    per = 384 // BZ
-    groups = flat.shape[0] // per
-    lane = lane_iota(groups)
-    r = [pltpu.roll(flat[pl.ds(k, groups, stride=per), :], BZ * k % LANES, 1) for k in range(per)]
-    for j in range(3):
-        tile = None
-        for k in range(per):
-            low, high = BZ * k - LANES * j, BZ * (k + 1) - LANES * j
-            if high > 0 and low < LANES:
-                tile = r[k] if tile is None else jnp.where(lane >= low, r[k], tile)
-        wide[pl.ds(j, groups, stride=3), :] = tile
-    tiles = BY * BZ // LANES
-    for t in range(tiles):
-        cut = slice(t * LANES, (t + 1) * LANES)
-        effective[:, cut] = wide[pl.ds(t, bx, stride=tiles), :]
-    for x in range(bx):
-        effective[x : x + 1, :] = effective[x : x + 1, :] + local_potential[x]
+    back = wide_dot(jnp.concatenate(pieces, 0), z_coarsen())
+    flat[...] = back
+    for x, row in enumerate(merge_rows(flat, wide)):
+        effective[x : x + 1, :] = row + local_part[x : x + 1, :]
 
     width, half = effective.shape[1], bands // 2
+    lane = lane_iota(half)
+    lane = jnp.concatenate([lane, lane], 0)
     spread = z_spread(cz)
-    lane = lane_iota(half)
+    z_faces = zf[...].reshape(bx * bands, LANES)
+    step = 2 * LANES
     stores = []
-    for x in range(bx):
-        outer = jnp.dot(zf[x], spread, preferred_element_type=F32)
-        low = high = None
-        for side, face in zip(y_sides, fld_y):
-            halo = -0.5 * face[x * half : (x + 1) * half, :].astype(F32)
-            if side != "hi":
-                here = jnp.concatenate([halo, pltpu.roll(halo, LANES - BZ, 1)], 0)
-                keep = jnp.concatenate([lane, lane], 0) < BZ
-                low = jnp.where(keep & (cy > 0), here, 0.0)
-            if side != "lo":
-                here = jnp.concatenate([pltpu.roll(halo, LANES - BZ, 1), pltpu.roll(halo, LANES - 2 * BZ, 1)], 0)
-                keep = jnp.concatenate([lane, lane], 0) >= LANES - BZ
-                high = jnp.where(keep & (cy < counts[1] - 1), here, 0.0)
-        for t in range(width // LANES):
-            cut = slice(t * LANES, (t + 1) * LANES)
-            total = inner[x, :, cut] + outer[:, cut] + effective[x : x + 1, cut] * orb[x, :, cut].astype(F32)
-            if t == 0:
-                total = total + low
-            if t == width // LANES - 1:
-                total = total + high
-            for side, face in zip(x_sides, x_faces):
-                if x == 0 and side != "hi":
-                    total = total + jnp.where(cx > 0, -0.5, 0.0) * face[:, cut].astype(F32)
-                if x == bx - 1 and side != "lo":
-                    total = total + jnp.where(cx < counts[0] - 1, -0.5, 0.0) * face[:, cut].astype(F32)
-            result[x, :, cut] = total.astype(BF16)
-        stores.append(pltpu.make_async_copy(result.at[x], out.at[x], store.at[x]))
+    for j in range(0, width, step):
+        columns = min(step, width - j)
+        outer = jnp.dot(z_faces, spread[:, j : j + columns], preferred_element_type=F32)
+        for x in range(bx):
+            for t in range(j, j + columns, LANES):
+                cut = slice(t, t + LANES)
+                total = inner[x, :, cut] + effective[x : x + 1, cut] * orb[x, :, cut].astype(F32)
+                total = total + outer[x * bands : (x + 1) * bands, t - j : t - j + LANES]
+                for side, face in zip(y_sides, fld_y):
+                    halo = -0.5 * face[x * half : (x + 1) * half, :].astype(F32)
+                    if t == 0 and side != "hi":
+                        here = jnp.concatenate([halo, pltpu.roll(halo, LANES - BZ, 1)], 0)
+                        total = total + jnp.where((lane < BZ) & (cy > 0), here, 0.0)
+                    if t == width - LANES and side != "lo":
+                        here = [pltpu.roll(halo, LANES - BZ, 1), pltpu.roll(halo, LANES - 2 * BZ, 1)]
+                        keep = (lane >= LANES - BZ) & (cy < counts[1] - 1)
+                        total = total + jnp.where(keep, jnp.concatenate(here, 0), 0.0)
+                for side, face in zip(x_sides, x_faces):
+                    if x == 0 and side != "hi":
+                        total = total + jnp.where(cx > 0, -0.5, 0.0) * face[:, cut].astype(F32)
+                    if x == bx - 1 and side != "lo":
+                        total = total + jnp.where(cx < counts[0] - 1, -0.5, 0.0) * face[:, cut].astype(F32)
+                result[x, :, cut] = total.astype(BF16)
+        cut = pl.ds(j, columns)
+        stores.append(pltpu.make_async_copy(result.at[:, :, cut], out.at[:, :, cut], store.at[j // step]))
         stores[-1].start()
     for copy in stores + [send_potential]:
         copy.wait()
@@ -507,7 +542,9 @@
         cost_estimate=pl.CostEstimate(flops=3 * 10**9, bytes_accessed=10**6, transcendentals=0),
         name="fields",
     )(orb, *flat, *mates)
-    fields = [fetch(r, counts, m) for r, m in zip(rims, moves)]
+    corner_rims = rims[len(x_sides) + len(y_sides) :]
+    fields = [fetch(r, counts, m) for r, m in zip(rims, moves) if list(m) == [0]]
+    fields += [fetch(r, counts, m) for r, m in zip(rims, moves) if list(m) == [1]]
 
     rho = pl.pallas_call(
         functools.partial(total_kernel, counts, 1.0 / (bands * groups)),
@@ -519,20 +556,30 @@
         name="total",
     )(*parts)
     mate = fetch(rho, counts, {2: "swap"})
-    cut_rows = [WC * BY] * len(x_sides) + [bx * PAD] * len(y_sides) + [(WC + 1) * PAD] * len(xy_sides)
+    corner_rows = (WC + 1) * PAD + (WV + WS + 1) * PAD
+    cut_rows = [WC * BY] * len(x_sides) + [bx * PAD] * len(y_sides) + [corner_rows] * len(xy_sides)
     chip, *cuts = pl.pallas_call(
         functools.partial(cut_kernel, counts),
-        in_specs=[vmem(), vmem()],
+        in_specs=[vmem()] * (2 + len(corner_rims)),
         out_specs=[vmem()] * (1 + len(cut_rows)),
         out_shape=[shape(bx * BY, LANES)] + [shape(n, LANES, dtype=BF16) for n in cut_rows],
         compiler_params=params(1024),
         name="cut",
-    )(rho, mate)
+    )(rho, mate, *corner_rims)
     densities = [fetch(c, counts, m) for c, m in zip(cuts, moves)]
 
     rc, ry, qx = BY + 2 * PAD, fy + 2 * PAD, fx + 2 * WV
     local_rows = jnp.transpose(local_potential, (1, 0, 2))
-    operands = [chip, ext, local_rows, orb, inner, z_face, *densities, *fields, *x_faces]
+    local_part = pl.pallas_call(
+        functools.partial(local_kernel, counts),
+        in_specs=[vmem(), vmem()],
+        out_specs=vmem(),
+        out_shape=shape(bx, width),
+        scratch_shapes=[pltpu.VMEM((bx * BY, LANES), F32), pltpu.VMEM((bx * tiles, LANES), F32)],
+        compiler_params=params(1024),
+        name="local",
+    )(chip, local_rows)
+    operands = [chip, ext, local_part, orb, inner, z_face, *densities, *fields, *x_faces]
     applied, potential = pl.pallas_call(
         functools.partial(finish_kernel, counts),
         in_specs=[vmem()] * len(operands),
@@ -548,7 +595,7 @@
             pltpu.VMEM((bx, width), F32),
             pltpu.VMEM(flat[0].shape, F32),
             pltpu.VMEM((bx, bands, width), BF16),
-            pltpu.SemaphoreType.DMA((bx,)),
+            pltpu.SemaphoreType.DMA((pl.cdiv(width, 2 * LANES),)),
             pltpu.SemaphoreType.DMA(()),
         ],
         out_shape=[shape(bx, bands, width, dtype=BF16), shape(*flat[0].shape)],

time: 40.7 us -> 39.6 us (0.973)
  starting transfers between devices: 16.8 us -> 13.9 us
  waiting for transfers between devices: 12.4 us -> 14.7 us
  Pallas kernels: 10.7 us -> 10.1 us
    ppermute x11 -> x10, starting transfers between devices: 10.7 us -> 7.78 us  [fetch(): return lax.ppermute(block, 'dom', pairs)]
    ppermute x11 -> x10, waiting for transfers between devices: 7.71 us -> 10.1 us  [fetch(): return lax.ppermute(block, 'dom', pairs)]
    pallas_call x1, Pallas kernels: 3.41 us -> 2.94 us  [step(): pl.pallas_call(functools.partial(density_kernel, counts), in_specs=[hbm,...]
  transfers between devices with their start and end apart: 14 -> 13, of which waited for: 6 -> 6; matrix products, arithmetic and copies ran while one was open for 0% -> 0% of each run, Pallas kernels for 15% -> 15%
where the time goes in v1:
time: 39.6 us; the launch traced here: 39.5 us
  waiting for transfers between devices  14.7 us (37%)
  starting transfers between devices  13.9 us (35%)
  Pallas kernels  10.1 us (26%)
  between operations  0.76 us (2%)
    ppermute x10, waiting for transfers between devices, fetch(): return lax.ppermute(block, 'dom', pairs)  10.1 us
    ppermute x10, starting transfers between devices, fetch(): return lax.ppermute(block, 'dom', pairs)  7.78 us
    ppermute x3, starting transfers between devices, step(): parts.append(lax.ppermute(part, 'band', route))  6.08 us
    ppermute x3, waiting for transfers between devices, step(): parts.append(lax.ppermute(part, 'band', route))  4.66 us
    pallas_call x1, Pallas kernels, step(): pl.pallas_call(functools.partial(finish_kernel, counts), in_specs=[vmem()...  4.28 us
    pallas_call x1, Pallas kernels, step(): pl.pallas_call(functools.partial(density_kernel, counts), in_specs=[hbm,...  2.94 us
    pallas_call x1, Pallas kernels, step(): pl.pallas_call(laplace_kernel, in_specs=[vmem()], out_specs=vmem(), out_s...  1.66 us
  transfers between devices with their start and end apart: 13, of which 6 were waited for; matrix products, arithmetic and copies ran while one was open for 0% of the time, Pallas kernels for 15%

profile of v1, /device:TPU:0, one launch (start us, length us, event | category | flops | bytes accessed | tf_op | source)
XLA Modules:
  0.0 39.5 jit_solution(15262403037039027917)
XLA Ops:
  0.6 0.0 copy-start.1
  0.6 0.0 copy-start.2
  0.7 0.6 %collective-permute-start.4 = (f32[432,128]{1,0:T(8,128)}, f32[432,128]{1,0:T(8,128)S(1)}, u32[]{:S(2)}, u32[]{:S(2)}) collective-permute-start(f32[432,128]{1,0:T(8,128)} %bitcast.12), channel_id=1, source_target_pairs={{4,0},{0,4},{12,8},{8,12},{20,16},{16,20},{28,24},{24,28},{5,1},{1... | collective-permute-start | bytes 663560 | tf_op jit(solution)/shard_map/ppermute | solution.py:38
  1.2 0.1 collective-permute-start.5
  1.3 2.9 %density.1 = (f32[54,128]{1,0:T(8,128)S(1)}, bf16[6,192,1152]{2,1,0:T(8,128)(2,1)S(1)}, bf16[6,192,128]{2,1,0:T(8,128)(2,1)S(1)}, bf16[192,1152]{1,0:T(8,128)(2,1)S(1)}) custom-call(bf16[6,192,1152]{2,1,0:T(8,128)(2,1)} %bitcast.16, f32[1,192]{1,0:T(1,128)} %bitcast.17), custom_call_target="tpu_custom_call" | custom-call | tf_op jit(solution)/shard_map/density/pallas_call | solution.py:504
  4.2 5.1 %collective-permute-start.2 = (f32[54,128]{1,0:T(8,128)S(1)}, f32[54,128]{1,0:T(8,128)S(1)}, u32[]{:S(2)}, u32[]{:S(2)}) collective-permute-start(f32[54,128]{1,0:T(8,128)S(1)} %get-tuple-element.16.refs_0_), channel_id=1, source_target_pairs={{0,3},{1,0},{2,1},{3,2},{4,7},{5,4},{6,5},{7,6},{8,11},{9,8},{10,9... | collective-permute-start | bytes 82952 | tf_op jit(solution)/shard_map/ppermute | solution.py:521
  9.3 0.0 collective-permute-start.1
  9.3 1.0 %collective-permute-start = (f32[54,128]{1,0:T(8,128)S(1)}, f32[54,128]{1,0:T(8,128)S(1)}, u32[]{:S(2)}, u32[]{:S(2)}) collective-permute-start(f32[54,128]{1,0:T(8,128)S(1)} %get-tuple-element.16.refs_0_), channel_id=1, source_target_pairs={{0,1},{1,2},{2,3},{3,0},{4,5},{5,6},{6,7},{7,4},{8,9},{9,10},{10,1... | collective-permute-start | bytes 82952 | tf_op jit(solution)/shard_map/ppermute | solution.py:521
  10.3 0.5 %collective-permute-done.2.refs_3_ = f32[54,128]{1,0:T(8,128)S(1)} collective-permute-done((f32[54,128]{1,0:T(8,128)S(1)}, f32[54,128]{1,0:T(8,128)S(1)}, u32[]{:S(2)}, u32[]{:S(2)}) %collective-permute-start.2) | collective-permute-done | bytes 27680 | tf_op jit(solution)/shard_map/ppermute | solution.py:521
  10.9 3.2 %collective-permute-done.1.refs_2_ = f32[54,128]{1,0:T(8,128)S(1)} collective-permute-done((f32[54,128]{1,0:T(8,128)S(1)}, f32[54,128]{1,0:T(8,128)S(1)}, u32[]{:S(2)}, u32[]{:S(2)}) %collective-permute-start.1) | collective-permute-done | bytes 27680 | tf_op jit(solution)/shard_map/ppermute | solution.py:521
  14.1 0.9 %collective-permute-done.refs_1_ = f32[54,128]{1,0:T(8,128)S(1)} collective-permute-done((f32[54,128]{1,0:T(8,128)S(1)}, f32[54,128]{1,0:T(8,128)S(1)}, u32[]{:S(2)}, u32[]{:S(2)}) %collective-permute-start) | collective-permute-done | bytes 27680 | tf_op jit(solution)/shard_map/ppermute | solution.py:521
  15.0 0.2 total.1.rho
  15.2 0.1 collective-permute-start.3
  15.2 0.0 collective-permute-done.4.mate_prev
  15.3 0.0 collective-permute-done.5.mate_comp
  15.3 0.0 copy-done.1
  15.3 0.0 copy-done.2
  15.3 0.8 %fields.1 = (f32[1152,128]{1,0:T(8,128)S(1)}, bf16[432,128]{1,0:T(8,128)(2,1)S(1)}, bf16[768,128]{1,0:T(8,128)(2,1)S(1)}, bf16[80,128]{1,0:T(8,128)(2,1)S(1)}) custom-call(bf16[6,192,1152]{2,1,0:T(8,128)(2,1)S(1)} %get-tuple-element.17.orb.refs_3_, f32[432,128]{1,0:T(8,128)S(1)} %bitcast.13, f32[432,128]{1,0:T(8,128)S(1)} %bitcast.15, ...), custom_call_target="tpu_custom_call" | custom-call | flops 3000000000 | bytes 1000000 | tf_op jit(solution)/shard_map/fields/pallas_call | solution.py:536
  16.1 0.4 %collective-permute-done.3.mate = f32[144,128]{1,0:T(8,128)S(1)} collective-permute-done((f32[144,128]{1,0:T(8,128)S(1)}, f32[144,128]{1,0:T(8,128)S(1)}, u32[]{:S(2)}, u32[]{:S(2)}) %collective-permute-start.3) | collective-permute-done | bytes 73760 | tf_op jit(solution)/shard_map/ppermute | solution.py:38
  16.5 1.6 %collective-permute-start.7 = (bf16[72,128]{1,0:T(8,128)(2,1)S(1)}, bf16[72,128]{1,0:T(8,128)(2,1)S(1)}, u32[]{:S(2)}, u32[]{:S(2)}) collective-permute-start(bf16[72,128]{1,0:T(8,128)(2,1)S(1)} %get-tuple-element.22), channel_id=1, source_target_pairs={{16,0},{20,4},{24,8},{28,12},{0,16},{4,20},{8,24},{12,28},{17,1},{... | collective-permute-start | bytes 55304 | tf_op jit(solution)/shard_map/ppermute | solution.py:38
  18.1 1.5 %collective-permute-start.8 = (bf16[48,128]{1,0:T(8,128)(2,1)S(1)}, bf16[48,128]{1,0:T(8,128)(2,1)S(1)}, u32[]{:S(2)}, u32[]{:S(2)}) collective-permute-start(bf16[48,128]{1,0:T(8,128)(2,1)S(1)} %get-tuple-element.23), channel_id=1, source_target_pairs={{8,0},{12,4},{0,8},{4,12},{24,16},{28,20},{16,24},{20,28},{9,1},{1... | collective-permute-start | bytes 36872 | tf_op jit(solution)/shard_map/ppermute | solution.py:38
  19.6 0.0 collective-permute-start.6
  19.6 0.5 %collective-permute-start.12 = (bf16[192,1152]{1,0:T(8,128)(2,1)S(1)}, bf16[192,1152]{1,0:T(8,128)(2,1)S(1)}, u32[]{:S(2)}, u32[]{:S(2)}) collective-permute-start(bf16[192,1152]{1,0:T(8,128)(2,1)S(1)} %get-tuple-element.27), channel_id=1, source_target_pairs={{16,0},{20,4},{24,8},{28,12},{0,16},{4,20},{8,24},{12,28},{17,1},{... | collective-permute-start | bytes 1327112 | tf_op jit(solution)/shard_map/ppermute | solution.py:38
  20.1 1.5 %collective-permute-start.9 = (bf16[112,128]{1,0:T(8,128)(2,1)S(1)}, bf16[112,128]{1,0:T(8,128)(2,1)S(1)}, u32[]{:S(2)}, u32[]{:S(2)}) collective-permute-start(bf16[112,128]{1,0:T(8,128)(2,1)S(1)} %get-tuple-element.24), channel_id=1, source_target_pairs={{24,0},{28,4},{16,8},{20,12},{8,16},{12,20},{0,24},{4,28},{25,1},{... | collective-permute-start | bytes 86024 | tf_op jit(solution)/shard_map/ppermute | solution.py:38
  21.6 0.2 collective-permute-done.8.refs_7_
  21.8 0.5 %collective-permute-start.10 = (bf16[432,128]{1,0:T(8,128)(2,1)S(1)}, bf16[432,128]{1,0:T(8,128)(2,1)S(1)}, u32[]{:S(2)}, u32[]{:S(2)}) collective-permute-start(bf16[432,128]{1,0:T(8,128)(2,1)S(1)} %get-tuple-element.25), channel_id=1, source_target_pairs={{16,0},{20,4},{24,8},{28,12},{0,16},{4,20},{8,24},{12,28},{17,1},{... | collective-permute-start | bytes 331784 | tf_op jit(solution)/shard_map/ppermute | solution.py:38
  22.3 0.0 collective-permute-done.7.refs_6_
  22.3 0.0 copy-start
  22.3 1.5 %collective-permute-start.11 = (bf16[768,128]{1,0:T(8,128)(2,1)S(1)}, bf16[768,128]{1,0:T(8,128)(2,1)S(1)}, u32[]{:S(2)}, u32[]{:S(2)}) collective-permute-start(bf16[768,128]{1,0:T(8,128)(2,1)S(1)} %get-tuple-element.26), channel_id=1, source_target_pairs={{8,0},{12,4},{0,8},{4,12},{24,16},{28,20},{16,24},{20,28},{9,1},{1... | collective-permute-start | bytes 589832 | tf_op jit(solution)/shard_map/ppermute | solution.py:38
  23.8 1.7 %laplace.1.refs_4_ = f32[6,192,1152]{2,1,0:T(8,128)S(1)} custom-call(bf16[6,192,1152]{2,1,0:T(8,128)(2,1)S(1)} %get-tuple-element.17.orb.refs_3_), custom_call_target="tpu_custom_call" | custom-call | flops 6000000000 | bytes 8000000 | tf_op jit(solution)/shard_map/laplace/pallas_call | solution.py:524
  25.5 0.0 copy-done
  25.5 0.3 local.1.refs_2_
  25.7 0.0 collective-permute-done.9.refs_8_
  25.8 0.0 collective-permute-done.6.refs_5_
  25.8 9.4 %collective-permute-done.10.refs_9_ = bf16[432,128]{1,0:T(8,128)(2,1)S(1)} collective-permute-done((bf16[432,128]{1,0:T(8,128)(2,1)S(1)}, bf16[432,128]{1,0:T(8,128)(2,1)S(1)}, u32[]{:S(2)}, u32[]{:S(2)}) %collective-permute-start.10) | collective-permute-done | bytes 110624 | tf_op jit(solution)/shard_map/ppermute | solution.py:38
  35.2 0.0 collective-permute-done.11.refs_10_
  35.2 0.0 collective-permute-done.12.refs_11_
  35.2 4.3 %finish.1 = (bf16[6,192,1152]{2,1,0:T(8,128)(2,1)}, f32[432,128]{1,0:T(8,128)}) custom-call(f32[144,128]{1,0:T(8,128)S(1)} %get-tuple-element.19.chip.refs_0_, f32[1152,128]{1,0:T(8,128)S(1)} %get-tuple-element.20.refs_1_, f32[6,1152]{1,0:T(8,128)S(1)} %local.1.refs_2_, bf16[6,192,1152]{2,1,0:T(8,128)(2,1)S(1)} %get-tuple-element.17.orb.refs_3_, ...), custom_call_target="tpu_custom_call" | custom-call | tf_op jit(solution)/shard_map/finish/pallas_call | solution.py:583
  (1 shorter events, 0.0 us)
Async XLA Ops:
  0.6 14.6 %copy-start.1 = (f32[1,12,4608]{2,0,1:T(1,128)S(1)}, f32[1,12,4608]{2,0,1:T(1,128)}, u32[]{:S(2)}) copy-start(f32[1,12,4608]{2,0,1:T(1,128)} %param.7) | copy-start | bytes 663556
  0.6 14.6 %copy-start.2 = (f32[1,12,4608]{2,0,1:T(1,128)S(1)}, f32[1,12,4608]{2,0,1:T(1,128)}, u32[]{:S(2)}) copy-start(f32[1,12,4608]{2,0,1:T(1,128)} %param.8) | copy-start | bytes 663556
  0.7 14.6 %collective-permute-start.4 = (f32[432,128]{1,0:T(8,128)}, f32[432,128]{1,0:T(8,128)S(1)}, u32[]{:S(2)}, u32[]{:S(2)}) collective-permute-start(f32[432,128]{1,0:T(8,128)} %bitcast.12), channel_id=1, source_target_pairs={{4,0},{0,4},{12,8},{8,12},{20,16},{16,20},{28,24},{24,28},{5,1},{1... | collective-permute-start | bytes 663560 | tf_op jit(solution)/shard_map/ppermute | solution.py:38
  1.2 14.1 %collective-permute-start.5 = (f32[432,128]{1,0:T(8,128)}, f32[432,128]{1,0:T(8,128)S(1)}, u32[]{:S(2)}, u32[]{:S(2)}) collective-permute-start(f32[432,128]{1,0:T(8,128)} %bitcast.14), channel_id=1, source_target_pairs={{4,0},{0,4},{12,8},{8,12},{20,16},{16,20},{28,24},{24,28},{5,1},{1... | collective-permute-start | bytes 663560 | tf_op jit(solution)/shard_map/ppermute | solution.py:38
  4.2 6.6 %collective-permute-start.2 = (f32[54,128]{1,0:T(8,128)S(1)}, f32[54,128]{1,0:T(8,128)S(1)}, u32[]{:S(2)}, u32[]{:S(2)}) collective-permute-start(f32[54,128]{1,0:T(8,128)S(1)} %get-tuple-element.16.refs_0_), channel_id=1, source_target_pairs={{0,3},{1,0},{2,1},{3,2},{4,7},{5,4},{6,5},{7,6},{8,11},{9,8},{10,9... | collective-permute-start | bytes 82952 | tf_op jit(solution)/shard_map/ppermute | solution.py:521
  9.3 4.8 %collective-permute-start.1 = (f32[54,128]{1,0:T(8,128)S(1)}, f32[54,128]{1,0:T(8,128)S(1)}, u32[]{:S(2)}, u32[]{:S(2)}) collective-permute-start(f32[54,128]{1,0:T(8,128)S(1)} %get-tuple-element.16.refs_0_), channel_id=1, source_target_pairs={{0,2},{1,3},{2,0},{3,1},{4,6},{5,7},{6,4},{7,5},{8,10},{9,11},{10,... | collective-permute-start | bytes 82952 | tf_op jit(solution)/shard_map/ppermute | solution.py:521
  9.3 5.7 %collective-permute-start = (f32[54,128]{1,0:T(8,128)S(1)}, f32[54,128]{1,0:T(8,128)S(1)}, u32[]{:S(2)}, u32[]{:S(2)}) collective-permute-start(f32[54,128]{1,0:T(8,128)S(1)} %get-tuple-element.16.refs_0_), channel_id=1, source_target_pairs={{0,1},{1,2},{2,3},{3,0},{4,5},{5,6},{6,7},{7,4},{8,9},{9,10},{10,1... | collective-permute-start | bytes 82952 | tf_op jit(solution)/shard_map/ppermute | solution.py:521
  15.2 1.3 %collective-permute-start.3 = (f32[144,128]{1,0:T(8,128)S(1)}, f32[144,128]{1,0:T(8,128)S(1)}, u32[]{:S(2)}, u32[]{:S(2)}) collective-permute-start(f32[144,128]{1,0:T(8,128)S(1)} %total.1.rho), channel_id=1, source_target_pairs={{4,0},{0,4},{12,8},{8,12},{20,16},{16,20},{28,24},{24,28},{5,1},{1... | collective-permute-start | bytes 221192 | tf_op jit(solution)/shard_map/ppermute | solution.py:38
  16.5 5.8 %collective-permute-start.7 = (bf16[72,128]{1,0:T(8,128)(2,1)S(1)}, bf16[72,128]{1,0:T(8,128)(2,1)S(1)}, u32[]{:S(2)}, u32[]{:S(2)}) collective-permute-start(bf16[72,128]{1,0:T(8,128)(2,1)S(1)} %get-tuple-element.22), channel_id=1, source_target_pairs={{16,0},{20,4},{24,8},{28,12},{0,16},{4,20},{8,24},{12,28},{17,1},{... | collective-permute-start | bytes 55304 | tf_op jit(solution)/shard_map/ppermute | solution.py:38
  18.1 3.7 %collective-permute-start.8 = (bf16[48,128]{1,0:T(8,128)(2,1)S(1)}, bf16[48,128]{1,0:T(8,128)(2,1)S(1)}, u32[]{:S(2)}, u32[]{:S(2)}) collective-permute-start(bf16[48,128]{1,0:T(8,128)(2,1)S(1)} %get-tuple-element.23), channel_id=1, source_target_pairs={{8,0},{12,4},{0,8},{4,12},{24,16},{28,20},{16,24},{20,28},{9,1},{1... | collective-permute-start | bytes 36872 | tf_op jit(solution)/shard_map/ppermute | solution.py:38
  19.6 6.2 %collective-permute-start.6 = (bf16[6,192,128]{2,1,0:T(8,128)(2,1)S(1)}, bf16[6,192,128]{2,1,0:T(8,128)(2,1)S(1)}, u32[]{:S(2)}, u32[]{:S(2)}) collective-permute-start(bf16[6,192,128]{2,1,0:T(8,128)(2,1)S(1)} %get-tuple-element.21), channel_id=1, source_target_pairs={{4,0},{0,4},{12,8},{8,12},{20,16},{16,20},{28,24},{24,28},{5,1},{1... | collective-permute-start | bytes 884744 | tf_op jit(solution)/shard_map/ppermute | solution.py:38
  19.6 15.6 %collective-permute-start.12 = (bf16[192,1152]{1,0:T(8,128)(2,1)S(1)}, bf16[192,1152]{1,0:T(8,128)(2,1)S(1)}, u32[]{:S(2)}, u32[]{:S(2)}) collective-permute-start(bf16[192,1152]{1,0:T(8,128)(2,1)S(1)} %get-tuple-element.27), channel_id=1, source_target_pairs={{16,0},{20,4},{24,8},{28,12},{0,16},{4,20},{8,24},{12,28},{17,1},{... | collective-permute-start | bytes 1327112 | tf_op jit(solution)/shard_map/ppermute | solution.py:38
  20.1 5.6 %collective-permute-start.9 = (bf16[112,128]{1,0:T(8,128)(2,1)S(1)}, bf16[112,128]{1,0:T(8,128)(2,1)S(1)}, u32[]{:S(2)}, u32[]{:S(2)}) collective-permute-start(bf16[112,128]{1,0:T(8,128)(2,1)S(1)} %get-tuple-element.24), channel_id=1, source_target_pairs={{24,0},{28,4},{16,8},{20,12},{8,16},{12,20},{0,24},{4,28},{25,1},{... | collective-permute-start | bytes 86024 | tf_op jit(solution)/shard_map/ppermute | solution.py:38
  21.8 13.4 %collective-permute-start.10 = (bf16[432,128]{1,0:T(8,128)(2,1)S(1)}, bf16[432,128]{1,0:T(8,128)(2,1)S(1)}, u32[]{:S(2)}, u32[]{:S(2)}) collective-permute-start(bf16[432,128]{1,0:T(8,128)(2,1)S(1)} %get-tuple-element.25), channel_id=1, source_target_pairs={{16,0},{20,4},{24,8},{28,12},{0,16},{4,20},{8,24},{12,28},{17,1},{... | collective-permute-start | bytes 331784 | tf_op jit(solution)/shard_map/ppermute | solution.py:38
  22.3 3.2 %copy-start = (f32[1,6,1152]{2,0,1:T(1,128)S(1)}, f32[1,6,1152]{2,0,1:T(1,128)}, u32[]{:S(2)}) copy-start(f32[1,6,1152]{2,0,1:T(1,128)} %param.9) | copy-start | bytes 82948
  22.3 12.9 %collective-permute-start.11 = (bf16[768,128]{1,0:T(8,128)(2,1)S(1)}, bf16[768,128]{1,0:T(8,128)(2,1)S(1)}, u32[]{:S(2)}, u32[]{:S(2)}) collective-permute-start(bf16[768,128]{1,0:T(8,128)(2,1)S(1)} %get-tuple-element.26), channel_id=1, source_target_pairs={{8,0},{12,4},{0,8},{4,12},{24,16},{28,20},{16,24},{20,28},{9,1},{1... | collective-permute-start | bytes 589832 | tf_op jit(solution)/shard_map/ppermute | solution.py:38

commit v2 on v1

--- a/solution.py
+++ b/solution.py
@@ -105,7 +105,8 @@
 
 
 def lanes_of(value, index):
-    return jnp.take_along_axis(value, index, axis=1, mode="promise_in_bounds")
+    pieces = [value[r : r + 8] for r in range(0, value.shape[0], 8)]
+    return [jnp.take_along_axis(p, index, axis=1, mode="promise_in_bounds") for p in pieces]
 
 
 def stencil(first, columns):
@@ -125,23 +126,24 @@
     return jnp.sum(value, axis=0, keepdims=True)
 
 
-def density_kernel(counts, orb, occ, part, held, zf, *refs):
-    x_faces, (weights, load, load_occ) = refs[:-3], refs[-3:]
+def density_kernel(counts, orb, occ, prev, comp, part, held, mate_sent, *refs):
+    x_faces, (weights, fields, load, load_occ, load_field) = refs[:-5], refs[-5:]
     planes, bands, width = held.shape
-    tiles = width // LANES
+    tiles, rows = width // LANES, prev.shape[0]
     pos = position(counts)
     first = pltpu.make_async_copy(occ, weights, load_occ)
     first.start()
     loads = [pltpu.make_async_copy(orb.at[x], held.at[x], load.at[x]) for x in range(planes)]
+    loads += [pltpu.make_async_copy(ref, fields.at[f], load_field.at[f]) for f, ref in enumerate((prev, comp))]
     for copy in loads:
         copy.start()
     split = min(4, tiles)
     pick = z_pick(pos[2], split * LANES)
-    face_lane = lane_iota(bands) * BZ + jnp.where(pos[2] == 0, BZ - 1, 0)
+    face_lane = lane_iota(8) * BZ + jnp.where(pos[2] == 0, BZ - 1, 0)
     first.wait()
-    rows = jnp.broadcast_to(weights[...], (LANES, bands))
-    rows = jnp.concatenate([rows, jnp.zeros((LANES, -bands % LANES), F32)], 1)
-    weight = jnp.concatenate([rows[:, b : b + LANES].T for b in range(0, bands, LANES)], 0)[:bands]
+    column = jnp.broadcast_to(weights[...], (LANES, bands))
+    column = jnp.concatenate([column, jnp.zeros((LANES, -bands % LANES), F32)], 1)
+    weight = jnp.concatenate([column[:, b : b + LANES].T for b in range(0, bands, LANES)], 0)[:bands]
     for x in range(planes):
         loads[x].wait()
         face = jnp.dot(held[x, :, : split * LANES], pick, preferred_element_type=F32)
@@ -150,10 +152,15 @@
             part[tiles * x + t : tiles * x + t + 1, :] = sum_rows(f * f * weight)
             if t >= split:
                 at = face_lane - t * LANES
-                face = jnp.where(at >= 0, lanes_of(f, at & (LANES - 1)), face)
-        zf[x] = face.astype(BF16)
+                got = lanes_of(f, at & (LANES - 1))
+                face = [jnp.where(at >= 0, new, face[8 * i : 8 * i + 8]) for i, new in enumerate(got)]
+                face = jnp.concatenate(face, 0)
+        mate_sent[2 * rows + x * bands : 2 * rows + (x + 1) * bands, :] = face.astype(BF16)
     for side, face in zip(sides(counts[0]), x_faces):
         face[...] = held[rim_start(side, pos[0], planes, 1)]
+    for f in range(2):
+        loads[planes + f].wait()
+        mate_sent[f * rows : (f + 1) * rows, :] = fields[f].astype(BF16)
 
 
 def total_kernel(counts, scale, *refs):
@@ -210,8 +217,9 @@
     )
 
 
-def field_kernel(counts, orb, prev, comp, mate_prev, mate_comp, ext, *refs):
-    sends, pos = list(refs), position(counts)
+def field_kernel(counts, orb, prev, comp, mate, ext, *refs):
+    sends, mate32, pos = list(refs[:-1]), refs[-1], position(counts)
+    mate32[...] = mate[: mate32.shape[0], :].astype(F32)
     bx, bands, row_lanes = orb.shape
     half = bands // 2
     fx, fy = prev.shape[0] * LANES // (2 * BY * 2 * BZ), 2 * BY
@@ -224,9 +232,9 @@
     edge_high = jnp.where(first, LANES, ZOFF)
     edge = (lane >= edge_low) & (lane < edge_high)
     rows = fx * fy
-    for f, (ref, mate) in enumerate(((prev, mate_prev), (comp, mate_comp))):
+    for f, ref in enumerate((prev, comp)):
         mine = field_rows(ref, groups)
-        theirs = field_rows(mate, groups)
+        theirs = field_rows(mate32.at[pl.ds(f * prev.shape[0], prev.shape[0])], groups)
         for k in range(4):
             halo = jnp.where(edge, pltpu.roll(theirs[k], shift, 1), 0.0)
             ext[pl.ds(f * rows + k, groups, stride=4), :] = jnp.where(own, mine[k], halo)
@@ -298,7 +306,7 @@
 
 def finish_kernel(counts, *refs):
     it = iter(refs)
-    chip, ext, local_part, orb, inner, zf = (next(it) for _ in range(6))
+    chip, ext, local_part, orb, inner, mate_block = (next(it) for _ in range(6))
     x_sides, y_sides = sides(counts[0]), sides(counts[1])
     xy_sides = [(a, b) for a in x_sides for b in y_sides]
     rho_x, rho_y, rho_xy = ([next(it) for _ in s] for s in (x_sides, y_sides, xy_sides))
@@ -421,7 +429,7 @@
     lane = lane_iota(half)
     lane = jnp.concatenate([lane, lane], 0)
     spread = z_spread(cz)
-    z_faces = zf[...].reshape(bx * bands, LANES)
+    z_faces = mate_block[2 * potential.shape[0] :, :]
     step = 2 * LANES
     stores = []
     for j in range(0, width, step):
@@ -498,28 +506,32 @@
         return pltpu.CompilerParams(vmem_limit_bytes=kib * 2**10)
 
     flat = [a.reshape(fx * fy * 2 * BZ // LANES, LANES) for a in (previous, compensation)]
-    mates = [fetch(a, counts, {2: "swap"}) for a in flat]
-
     orb = jnp.transpose(orbitals.reshape(bands, bx, width), (1, 0, 2))
-    part, orb, z_face, *x_faces = pl.pallas_call(
+    mate_rows = 2 * flat[0].shape[0] + bx * bands
+    inputs = [orb, occupations.reshape(1, bands), *flat]
+    part, orb, mate_block, *x_faces = pl.pallas_call(
         functools.partial(density_kernel, counts),
-        in_specs=[hbm, hbm],
+        in_specs=[hbm] * 4,
         out_specs=[vmem()] * (3 + len(x_sides)),
-        out_shape=[shape(bx * tiles, LANES), shape(*orb.shape, dtype=BF16), shape(bx, bands, LANES, dtype=BF16)]
+        out_shape=[shape(bx * tiles, LANES), shape(*orb.shape, dtype=BF16)]
+        + [shape(mate_rows, LANES, dtype=BF16)]
         + [shape(bands, width, dtype=BF16) for _ in x_sides],
-        scratch_shapes=[pltpu.VMEM((1, bands), F32), pltpu.SemaphoreType.DMA((bx,)), pltpu.SemaphoreType.DMA(())],
+        scratch_shapes=[
+            pltpu.VMEM((1, bands), F32),
+            pltpu.VMEM((2, *flat[0].shape), F32),
+            pltpu.SemaphoreType.DMA((bx,)),
+            pltpu.SemaphoreType.DMA(()),
+            pltpu.SemaphoreType.DMA((2,)),
+        ],
         compiler_params=params(8 * 1024),
         name="density",
-    )(
-        pltpu.with_memory_space_constraint(orb, pltpu.HBM),
-        pltpu.with_memory_space_constraint(occupations.reshape(1, bands), pltpu.HBM),
-    )
+    )(*(pltpu.with_memory_space_constraint(a, pltpu.HBM) for a in inputs))
     x_faces = [fetch(f, counts, {0: s}) for s, f in zip(x_sides, x_faces)]
+    mate_block = fetch(mate_block, counts, {2: "swap"})
     parts = [part]
     for shift in range(1, groups):
-        route = [(i, (i + shift) % groups) for i in range(groups)]
+        route = [(i, i ^ shift if groups & (groups - 1) == 0 else (i + shift) % groups) for i in range(groups)]
         parts.append(lax.ppermute(part, "band", route))
-    z_face = fetch(z_face, counts, {2: "swap"})
 
     inner = pl.pallas_call(
         laplace_kernel,
@@ -535,13 +547,14 @@
     rim_rows += [(WV + WS + 1) * PAD] * len(xy_sides)
     ext, *rims = pl.pallas_call(
         functools.partial(field_kernel, counts),
-        in_specs=[vmem()] * 5,
+        in_specs=[vmem()] * 4,
         out_specs=[vmem()] * (1 + len(rim_rows)),
         out_shape=[shape(2 * fx * fy, LANES)] + [shape(n, LANES, dtype=BF16) for n in rim_rows],
+        scratch_shapes=[pltpu.VMEM((2 * flat[0].shape[0], LANES), F32)],
         compiler_params=params(4 * 1024),
         cost_estimate=pl.CostEstimate(flops=3 * 10**9, bytes_accessed=10**6, transcendentals=0),
         name="fields",
-    )(orb, *flat, *mates)
+    )(orb, *flat, mate_block)
     corner_rims = rims[len(x_sides) + len(y_sides) :]
     fields = [fetch(r, counts, m) for r, m in zip(rims, moves) if list(m) == [0]]
     fields += [fetch(r, counts, m) for r, m in zip(rims, moves) if list(m) == [1]]
@@ -579,7 +592,7 @@
         compiler_params=params(1024),
         name="local",
     )(chip, local_rows)
-    operands = [chip, ext, local_part, orb, inner, z_face, *densities, *fields, *x_faces]
+    operands = [chip, ext, local_part, orb, inner, mate_block, *densities, *fields, *x_faces]
     applied, potential = pl.pallas_call(
         functools.partial(finish_kernel, counts),
         in_specs=[vmem()] * len(operands),

time: 39.6 us -> 31.4 us (0.79)
  waiting for transfers between devices: 14.7 us -> 7.23 us
  starting transfers between devices: 13.9 us -> 13.2 us
    ppermute x10 -> x8, waiting for transfers between devices: 10.1 us -> 3.25 us  [fetch(): return lax.ppermute(block, 'dom', pairs)]
    ppermute x3, starting transfers between devices: 6.08 us -> 4.39 us  [step(): parts.append(lax.ppermute(part, 'band', route))]
    ppermute x10 -> x8, starting transfers between devices: 7.78 us -> 8.77 us  [fetch(): return lax.ppermute(block, 'dom', pairs)]
    ppermute x3, waiting for transfers between devices: 4.66 us -> 3.98 us  [step(): parts.append(lax.ppermute(part, 'band', route))]
  transfers between devices with their start and end apart: 13 -> 11, of which waited for: 6 -> 5; matrix products, arithmetic and copies ran while one was open for 0% -> 0% of each run, Pallas kernels for 15% -> 9%
where the time goes in v2:
time: 31.4 us; the launch traced here: 31.3 us
  starting transfers between devices  13.2 us (42%)
  Pallas kernels  10.1 us (32%)
  waiting for transfers between devices  7.23 us (23%)
  between operations  0.76 us (2%)
    ppermute x8, starting transfers between devices, fetch(): return lax.ppermute(block, 'dom', pairs)  8.77 us
    ppermute x3, starting transfers between devices, step(): parts.append(lax.ppermute(part, 'band', route))  4.39 us
    pallas_call x1, Pallas kernels, step(): pl.pallas_call(functools.partial(finish_kernel, counts), in_specs=[vmem()...  4.23 us
    ppermute x3, waiting for transfers between devices, step(): parts.append(lax.ppermute(part, 'band', route))  3.98 us
    ppermute x8, waiting for transfers between devices, fetch(): return lax.ppermute(block, 'dom', pairs)  3.25 us
    pallas_call x1, Pallas kernels, step(): pl.pallas_call(functools.partial(density_kernel, counts), in_specs=[hbm]...  3.11 us
    pallas_call x1, Pallas kernels, step(): pl.pallas_call(laplace_kernel, in_specs=[vmem()], out_specs=vmem(), out_s...  1.66 us
    pallas_call x1, Pallas kernels, step(): pl.pallas_call(functools.partial(field_kernel, counts), in_specs=[vmem()]...  0.66 us
  transfers between devices with their start and end apart: 11, of which 5 were waited for; matrix products, arithmetic and copies ran while one was open for 0% of the time, Pallas kernels for 9%

profile of v2, /device:TPU:0, one launch (start us, length us, event | category | flops | bytes accessed | tf_op | source)
XLA Modules:
  0.0 31.3 jit_solution(9420616873326215167)
XLA Ops:
  0.6 0.0 copy-start.1
  0.6 0.0 copy-start
  0.7 3.1 %density.1 = (f32[54,128]{1,0:T(8,128)S(1)}, bf16[6,192,1152]{2,1,0:T(8,128)(2,1)S(1)}, bf16[2016,128]{1,0:T(8,128)(2,1)S(1)}, bf16[192,1152]{1,0:T(8,128)(2,1)S(1)}) custom-call(bf16[6,192,1152]{2,1,0:T(8,128)(2,1)} %bitcast.16, f32[1,192]{1,0:T(1,128)} %bitcast.17, f32[432,128]{1,0:T(8,128)} %bitcast.11, f32[432,128]{1,0:T(8,128)} %bitcast.13), custom_call_target="tpu_custom_call" | custom-call | tf_op jit(solution)/shard_map/density/pallas_call | solution.py:512
  3.8 0.6 %collective-permute-start.4 = (bf16[2016,128]{1,0:T(8,128)(2,1)S(1)}, bf16[2016,128]{1,0:T(8,128)(2,1)S(1)}, u32[]{:S(2)}, u32[]{:S(2)}) collective-permute-start(bf16[2016,128]{1,0:T(8,128)(2,1)S(1)} %get-tuple-element.18), channel_id=1, source_target_pairs={{4,0},{0,4},{12,8},{8,12},{20,16},{16,20},{28,24},{24,28},{5,1},{1... | collective-permute-start | bytes 1548296 | tf_op jit(solution)/shard_map/ppermute | solution.py:38
  4.3 2.6 %collective-permute-start.10 = (bf16[192,1152]{1,0:T(8,128)(2,1)S(1)}, bf16[192,1152]{1,0:T(8,128)(2,1)S(1)}, u32[]{:S(2)}, u32[]{:S(2)}) collective-permute-start(bf16[192,1152]{1,0:T(8,128)(2,1)S(1)} %get-tuple-element.27), channel_id=1, source_target_pairs={{16,0},{20,4},{24,8},{28,12},{0,16},{4,20},{8,24},{12,28},{17,1},{... | collective-permute-start | bytes 1327112 | tf_op jit(solution)/shard_map/ppermute | solution.py:38
  6.9 3.6 %collective-permute-start.2 = (f32[54,128]{1,0:T(8,128)S(1)}, f32[54,128]{1,0:T(8,128)S(1)}, u32[]{:S(2)}, u32[]{:S(2)}) collective-permute-start(f32[54,128]{1,0:T(8,128)S(1)} %get-tuple-element.16.refs_0_), channel_id=1, source_target_pairs={{0,3},{1,2},{2,1},{3,0},{4,7},{5,6},{6,5},{7,4},{8,11},{9,10},{10,... | collective-permute-start | bytes 82952 | tf_op jit(solution)/shard_map/ppermute | solution.py:534
  10.5 0.0 collective-permute-start.1
  10.5 0.8 %collective-permute-start = (f32[54,128]{1,0:T(8,128)S(1)}, f32[54,128]{1,0:T(8,128)S(1)}, u32[]{:S(2)}, u32[]{:S(2)}) collective-permute-start(f32[54,128]{1,0:T(8,128)S(1)} %get-tuple-element.16.refs_0_), channel_id=1, source_target_pairs={{0,1},{1,0},{2,3},{3,2},{4,5},{5,4},{6,7},{7,6},{8,9},{9,8},{10,11... | collective-permute-start | bytes 82952 | tf_op jit(solution)/shard_map/ppermute | solution.py:534
  11.3 1.3 %collective-permute-done.2.refs_3_ = f32[54,128]{1,0:T(8,128)S(1)} collective-permute-done((f32[54,128]{1,0:T(8,128)S(1)}, f32[54,128]{1,0:T(8,128)S(1)}, u32[]{:S(2)}, u32[]{:S(2)}) %collective-permute-start.2) | collective-permute-done | bytes 27680 | tf_op jit(solution)/shard_map/ppermute | solution.py:534
  12.6 2.7 %collective-permute-done.1.refs_2_ = f32[54,128]{1,0:T(8,128)S(1)} collective-permute-done((f32[54,128]{1,0:T(8,128)S(1)}, f32[54,128]{1,0:T(8,128)S(1)}, u32[]{:S(2)}, u32[]{:S(2)}) %collective-permute-start.1) | collective-permute-done | bytes 27680 | tf_op jit(solution)/shard_map/ppermute | solution.py:534
  15.3 0.0 collective-permute-done.refs_1_
  15.3 0.2 total.1.rho
  15.5 0.1 collective-permute-start.3
  15.5 0.0 collective-permute-done.4.mate.refs_5_
  15.6 0.0 copy-done.1
  15.6 0.0 copy-done
  15.6 0.7 %fields.1 = (f32[1152,128]{1,0:T(8,128)S(1)}, bf16[432,128]{1,0:T(8,128)(2,1)S(1)}, bf16[768,128]{1,0:T(8,128)(2,1)S(1)}, bf16[80,128]{1,0:T(8,128)(2,1)S(1)}) custom-call(bf16[6,192,1152]{2,1,0:T(8,128)(2,1)S(1)} %get-tuple-element.17.orb.refs_3_, f32[432,128]{1,0:T(8,128)S(1)} %bitcast.12, f32[432,128]{1,0:T(8,128)S(1)} %bitcast.14, ...), custom_call_target="tpu_custom_call" | custom-call | flops 3000000000 | bytes 1000000 | tf_op jit(solution)/shard_map/fields/pallas_call | solution.py:548
  16.2 0.6 %collective-permute-done.3.mate = f32[144,128]{1,0:T(8,128)S(1)} collective-permute-done((f32[144,128]{1,0:T(8,128)S(1)}, f32[144,128]{1,0:T(8,128)S(1)}, u32[]{:S(2)}, u32[]{:S(2)}) %collective-permute-start.3) | collective-permute-done | bytes 73760 | tf_op jit(solution)/shard_map/ppermute | solution.py:38
  16.8 1.6 %collective-permute-start.6 = (bf16[48,128]{1,0:T(8,128)(2,1)S(1)}, bf16[48,128]{1,0:T(8,128)(2,1)S(1)}, u32[]{:S(2)}, u32[]{:S(2)}) collective-permute-start(bf16[48,128]{1,0:T(8,128)(2,1)S(1)} %get-tuple-element.23), channel_id=1, source_target_pairs={{8,0},{12,4},{0,8},{4,12},{24,16},{28,20},{16,24},{20,28},{9,1},{1... | collective-permute-start | bytes 36872 | tf_op jit(solution)/shard_map/ppermute | solution.py:38
  18.4 0.5 %collective-permute-start.5 = (bf16[72,128]{1,0:T(8,128)(2,1)S(1)}, bf16[72,128]{1,0:T(8,128)(2,1)S(1)}, u32[]{:S(2)}, u32[]{:S(2)}) collective-permute-start(bf16[72,128]{1,0:T(8,128)(2,1)S(1)} %get-tuple-element.22), channel_id=1, source_target_pairs={{16,0},{20,4},{24,8},{28,12},{0,16},{4,20},{8,24},{12,28},{17,1},{... | collective-permute-start | bytes 55304 | tf_op jit(solution)/shard_map/ppermute | solution.py:38
  18.9 1.5 %collective-permute-start.7 = (bf16[112,128]{1,0:T(8,128)(2,1)S(1)}, bf16[112,128]{1,0:T(8,128)(2,1)S(1)}, u32[]{:S(2)}, u32[]{:S(2)}) collective-permute-start(bf16[112,128]{1,0:T(8,128)(2,1)S(1)} %get-tuple-element.24), channel_id=1, source_target_pairs={{24,0},{28,4},{16,8},{20,12},{8,16},{12,20},{0,24},{4,28},{25,1},{... | collective-permute-start | bytes 86024 | tf_op jit(solution)/shard_map/ppermute | solution.py:38
  20.4 0.5 %collective-permute-start.8 = (bf16[432,128]{1,0:T(8,128)(2,1)S(1)}, bf16[432,128]{1,0:T(8,128)(2,1)S(1)}, u32[]{:S(2)}, u32[]{:S(2)}) collective-permute-start(bf16[432,128]{1,0:T(8,128)(2,1)S(1)} %get-tuple-element.25), channel_id=1, source_target_pairs={{16,0},{20,4},{24,8},{28,12},{0,16},{4,20},{8,24},{12,28},{17,1},{... | collective-permute-start | bytes 331784 | tf_op jit(solution)/shard_map/ppermute | solution.py:38
  20.9 0.0 collective-permute-done.10.refs_11_
  20.9 0.0 copy-start.2
  20.9 1.5 %collective-permute-start.9 = (bf16[768,128]{1,0:T(8,128)(2,1)S(1)}, bf16[768,128]{1,0:T(8,128)(2,1)S(1)}, u32[]{:S(2)}, u32[]{:S(2)}) collective-permute-start(bf16[768,128]{1,0:T(8,128)(2,1)S(1)} %get-tuple-element.26), channel_id=1, source_target_pairs={{8,0},{12,4},{0,8},{4,12},{24,16},{28,20},{16,24},{20,28},{9,1},{1... | collective-permute-start | bytes 589832 | tf_op jit(solution)/shard_map/ppermute | solution.py:38
  22.4 1.7 %laplace.1.refs_4_ = f32[6,192,1152]{2,1,0:T(8,128)S(1)} custom-call(bf16[6,192,1152]{2,1,0:T(8,128)(2,1)S(1)} %get-tuple-element.17.orb.refs_3_), custom_call_target="tpu_custom_call" | custom-call | flops 6000000000 | bytes 8000000 | tf_op jit(solution)/shard_map/laplace/pallas_call | solution.py:536
  24.1 0.0 copy-done.2
  24.1 0.3 local.1.refs_2_
  24.3 0.0 collective-permute-done.6.refs_7_
  24.3 0.0 collective-permute-done.5.refs_6_
  24.3 0.0 collective-permute-done.7.refs_8_
  24.4 0.8 %collective-permute-done.8.refs_9_ = bf16[432,128]{1,0:T(8,128)(2,1)S(1)} collective-permute-done((bf16[432,128]{1,0:T(8,128)(2,1)S(1)}, bf16[432,128]{1,0:T(8,128)(2,1)S(1)}, u32[]{:S(2)}, u32[]{:S(2)}) %collective-permute-start.8) | collective-permute-done | bytes 110624 | tf_op jit(solution)/shard_map/ppermute | solution.py:38
  25.1 1.9 %collective-permute-done.9.refs_10_ = bf16[768,128]{1,0:T(8,128)(2,1)S(1)} collective-permute-done((bf16[768,128]{1,0:T(8,128)(2,1)S(1)}, bf16[768,128]{1,0:T(8,128)(2,1)S(1)}, u32[]{:S(2)}, u32[]{:S(2)}) %collective-permute-start.9) | collective-permute-done | bytes 196640 | tf_op jit(solution)/shard_map/ppermute | solution.py:38
  27.0 4.2 %finish.1 = (bf16[6,192,1152]{2,1,0:T(8,128)(2,1)}, f32[432,128]{1,0:T(8,128)}) custom-call(f32[144,128]{1,0:T(8,128)S(1)} %get-tuple-element.20.chip.refs_0_, f32[1152,128]{1,0:T(8,128)S(1)} %get-tuple-element.21.refs_1_, f32[6,1152]{1,0:T(8,128)S(1)} %local.1.refs_2_, bf16[6,192,1152]{2,1,0:T(8,128)(2,1)S(1)} %get-tuple-element.17.orb.refs_3_, ...), custom_call_target="tpu_custom_call" | custom-call | tf_op jit(solution)/shard_map/finish/pallas_call | solution.py:596
  (1 shorter events, 0.0 us)
Async XLA Ops:
  0.6 14.9 %copy-start.1 = (f32[1,12,4608]{2,0,1:T(1,128)S(1)}, f32[1,12,4608]{2,0,1:T(1,128)}, u32[]{:S(2)}) copy-start(f32[1,12,4608]{2,0,1:T(1,128)} %param.8) | copy-start | bytes 663556
  0.6 14.9 %copy-start = (f32[1,12,4608]{2,0,1:T(1,128)S(1)}, f32[1,12,4608]{2,0,1:T(1,128)}, u32[]{:S(2)}) copy-start(f32[1,12,4608]{2,0,1:T(1,128)} %param.7) | copy-start | bytes 663556
  3.8 11.8 %collective-permute-start.4 = (bf16[2016,128]{1,0:T(8,128)(2,1)S(1)}, bf16[2016,128]{1,0:T(8,128)(2,1)S(1)}, u32[]{:S(2)}, u32[]{:S(2)}) collective-permute-start(bf16[2016,128]{1,0:T(8,128)(2,1)S(1)} %get-tuple-element.18), channel_id=1, source_target_pairs={{4,0},{0,4},{12,8},{8,12},{20,16},{16,20},{28,24},{24,28},{5,1},{1... | collective-permute-start | bytes 1548296 | tf_op jit(solution)/shard_map/ppermute | solution.py:38
  4.3 16.6 %collective-permute-start.10 = (bf16[192,1152]{1,0:T(8,128)(2,1)S(1)}, bf16[192,1152]{1,0:T(8,128)(2,1)S(1)}, u32[]{:S(2)}, u32[]{:S(2)}) collective-permute-start(bf16[192,1152]{1,0:T(8,128)(2,1)S(1)} %get-tuple-element.27), channel_id=1, source_target_pairs={{16,0},{20,4},{24,8},{28,12},{0,16},{4,20},{8,24},{12,28},{17,1},{... | collective-permute-start | bytes 1327112 | tf_op jit(solution)/shard_map/ppermute | solution.py:38
  6.9 5.7 %collective-permute-start.2 = (f32[54,128]{1,0:T(8,128)S(1)}, f32[54,128]{1,0:T(8,128)S(1)}, u32[]{:S(2)}, u32[]{:S(2)}) collective-permute-start(f32[54,128]{1,0:T(8,128)S(1)} %get-tuple-element.16.refs_0_), channel_id=1, source_target_pairs={{0,3},{1,2},{2,1},{3,0},{4,7},{5,6},{6,5},{7,4},{8,11},{9,10},{10,... | collective-permute-start | bytes 82952 | tf_op jit(solution)/shard_map/ppermute | solution.py:534
  10.5 4.8 %collective-permute-start.1 = (f32[54,128]{1,0:T(8,128)S(1)}, f32[54,128]{1,0:T(8,128)S(1)}, u32[]{:S(2)}, u32[]{:S(2)}) collective-permute-start(f32[54,128]{1,0:T(8,128)S(1)} %get-tuple-element.16.refs_0_), channel_id=1, source_target_pairs={{0,2},{1,3},{2,0},{3,1},{4,6},{5,7},{6,4},{7,5},{8,10},{9,11},{10,... | collective-permute-start | bytes 82952 | tf_op jit(solution)/shard_map/ppermute | solution.py:534
  10.5 4.8 %collective-permute-start = (f32[54,128]{1,0:T(8,128)S(1)}, f32[54,128]{1,0:T(8,128)S(1)}, u32[]{:S(2)}, u32[]{:S(2)}) collective-permute-start(f32[54,128]{1,0:T(8,128)S(1)} %get-tuple-element.16.refs_0_), channel_id=1, source_target_pairs={{0,1},{1,0},{2,3},{3,2},{4,5},{5,4},{6,7},{7,6},{8,9},{9,8},{10,11... | collective-permute-start | bytes 82952 | tf_op jit(solution)/shard_map/ppermute | solution.py:534
  15.5 1.3 %collective-permute-start.3 = (f32[144,128]{1,0:T(8,128)S(1)}, f32[144,128]{1,0:T(8,128)S(1)}, u32[]{:S(2)}, u32[]{:S(2)}) collective-permute-start(f32[144,128]{1,0:T(8,128)S(1)} %total.1.rho), channel_id=1, source_target_pairs={{4,0},{0,4},{12,8},{8,12},{20,16},{16,20},{28,24},{24,28},{5,1},{1... | collective-permute-start | bytes 221192 | tf_op jit(solution)/shard_map/ppermute | solution.py:38
  16.8 7.5 %collective-permute-start.6 = (bf16[48,128]{1,0:T(8,128)(2,1)S(1)}, bf16[48,128]{1,0:T(8,128)(2,1)S(1)}, u32[]{:S(2)}, u32[]{:S(2)}) collective-permute-start(bf16[48,128]{1,0:T(8,128)(2,1)S(1)} %get-tuple-element.23), channel_id=1, source_target_pairs={{8,0},{12,4},{0,8},{4,12},{24,16},{28,20},{16,24},{20,28},{9,1},{1... | collective-permute-start | bytes 36872 | tf_op jit(solution)/shard_map/ppermute | solution.py:38
  18.4 6.0 %collective-permute-start.5 = (bf16[72,128]{1,0:T(8,128)(2,1)S(1)}, bf16[72,128]{1,0:T(8,128)(2,1)S(1)}, u32[]{:S(2)}, u32[]{:S(2)}) collective-permute-start(bf16[72,128]{1,0:T(8,128)(2,1)S(1)} %get-tuple-element.22), channel_id=1, source_target_pairs={{16,0},{20,4},{24,8},{28,12},{0,16},{4,20},{8,24},{12,28},{17,1},{... | collective-permute-start | bytes 55304 | tf_op jit(solution)/shard_map/ppermute | solution.py:38
  18.9 5.5 %collective-permute-start.7 = (bf16[112,128]{1,0:T(8,128)(2,1)S(1)}, bf16[112,128]{1,0:T(8,128)(2,1)S(1)}, u32[]{:S(2)}, u32[]{:S(2)}) collective-permute-start(bf16[112,128]{1,0:T(8,128)(2,1)S(1)} %get-tuple-element.24), channel_id=1, source_target_pairs={{24,0},{28,4},{16,8},{20,12},{8,16},{12,20},{0,24},{4,28},{25,1},{... | collective-permute-start | bytes 86024 | tf_op jit(solution)/shard_map/ppermute | solution.py:38
  20.4 4.7 %collective-permute-start.8 = (bf16[432,128]{1,0:T(8,128)(2,1)S(1)}, bf16[432,128]{1,0:T(8,128)(2,1)S(1)}, u32[]{:S(2)}, u32[]{:S(2)}) collective-permute-start(bf16[432,128]{1,0:T(8,128)(2,1)S(1)} %get-tuple-element.25), channel_id=1, source_target_pairs={{16,0},{20,4},{24,8},{28,12},{0,16},{4,20},{8,24},{12,28},{17,1},{... | collective-permute-start | bytes 331784 | tf_op jit(solution)/shard_map/ppermute | solution.py:38
  20.9 3.2 %copy-start.2 = (f32[1,6,1152]{2,0,1:T(1,128)S(1)}, f32[1,6,1152]{2,0,1:T(1,128)}, u32[]{:S(2)}) copy-start(f32[1,6,1152]{2,0,1:T(1,128)} %param.9) | copy-start | bytes 82948
  20.9 6.2 %collective-permute-start.9 = (bf16[768,128]{1,0:T(8,128)(2,1)S(1)}, bf16[768,128]{1,0:T(8,128)(2,1)S(1)}, u32[]{:S(2)}, u32[]{:S(2)}) collective-permute-start(bf16[768,128]{1,0:T(8,128)(2,1)S(1)} %get-tuple-element.26), channel_id=1, source_target_pairs={{8,0},{12,4},{0,8},{4,12},{24,16},{28,20},{16,24},{20,28},{9,1},{1... | collective-permute-start | bytes 589832 | tf_op jit(solution)/shard_map/ppermute | solution.py:38

commit v3 on v2

--- a/solution.py
+++ b/solution.py
@@ -94,9 +94,21 @@
     return jnp.where((step == 1) | (step == -1), 1.0, 0.0).astype(BF16)
 
 
+def z_columns(core, rows):
+    lane = lane_iota(rows)
+    at = BZ * (lane % BY) + jnp.where(core == 0, BZ - 1 - lane // BY, lane // BY)
+    return jnp.where(lane < WC * BY, at, -1)
+
+
 def z_pick(core, lanes):
-    lane, y = grid2(lanes, LANES)
-    return jnp.where(lane == BZ * y + jnp.where(core == 0, BZ - 1, 0), 1.0, 0.0).astype(BF16)
+    lane, _ = grid2(lanes, LANES)
+    return jnp.where(lane == z_columns(core, 1), 1.0, 0.0).astype(BF16)
+
+
+def z_place(core):
+    column, lane = grid2(LANES, LANES)
+    z = jnp.where(core == 0, BZ + column // BY, BZ - 1 - column // BY)
+    return jnp.where((lane == z) & (column < WC * BY), 1.0, 0.0).astype(BF16)
 
 
 def z_spread(core):
@@ -126,7 +138,7 @@
     return jnp.sum(value, axis=0, keepdims=True)
 
 
-def density_kernel(counts, orb, occ, prev, comp, part, held, mate_sent, *refs):
+def density_kernel(counts, orb, occ, prev, comp, part, held, mate_sent, weight_out, *refs):
     x_faces, (weights, fields, load, load_occ, load_field) = refs[:-5], refs[-5:]
     planes, bands, width = held.shape
     tiles, rows = width // LANES, prev.shape[0]
@@ -139,11 +151,12 @@
         copy.start()
     split = min(4, tiles)
     pick = z_pick(pos[2], split * LANES)
-    face_lane = lane_iota(8) * BZ + jnp.where(pos[2] == 0, BZ - 1, 0)
+    face_lane = z_columns(pos[2], 8)
     first.wait()
     column = jnp.broadcast_to(weights[...], (LANES, bands))
     column = jnp.concatenate([column, jnp.zeros((LANES, -bands % LANES), F32)], 1)
     weight = jnp.concatenate([column[:, b : b + LANES].T for b in range(0, bands, LANES)], 0)[:bands]
+    weight_out[...] = weight
     for x in range(planes):
         loads[x].wait()
         face = jnp.dot(held[x, :, : split * LANES], pick, preferred_element_type=F32)
@@ -163,16 +176,30 @@
         mate_sent[f * rows : (f + 1) * rows, :] = fields[f].astype(BF16)
 
 
-def total_kernel(counts, scale, *refs):
-    parts, out, flat = refs[:-2], refs[-2], refs[-1]
+def strip_kernel(part, mate, weight, out):
+    rows, bands = part.shape[0], weight.shape[0]
+    out[:rows, :] = part[...]
+    for x in range(out.shape[0] - rows):
+        start = mate.shape[0] - (out.shape[0] - rows - x) * bands
+        f = mate[start : start + bands, :].astype(F32)
+        out[rows + x : rows + x + 1, :] = sum_rows(f * f * weight[...])
+
+
+def total_kernel(counts, scale, bands_parts, *refs):
+    parts, refs = refs[:bands_parts], refs[bands_parts:]
+    x_sides, y_sides = sides(counts[0]), sides(counts[1])
+    corners = len(x_sides) * len(y_sides)
+    fields, chip, sends, flat = list(refs[:corners]), refs[corners], list(refs[corners + 1 : -1]), refs[-1]
+    cx, cy, cz = position(counts)
     total = parts[0][...]
     for part in parts[1:]:
         total = total + part[...]
     flat[...] = total * scale
     per = 384 // BZ
-    groups = flat.shape[0] // 3
+    bx = chip.shape[0] // BY
+    groups = chip.shape[0] // per
     lane = lane_iota(groups)
-    shift = jnp.where(position(counts)[2] == 0, 0, BZ)
+    shift = jnp.where(cz == 0, 0, BZ)
     tile = [flat[pl.ds(j, groups, stride=3), :] for j in range(3)]
     for k in range(per):
         at, off = divmod(BZ * k, LANES)
@@ -180,16 +207,11 @@
         if off + BZ > LANES:
             row = jnp.where(lane < LANES - off, row, pltpu.roll(tile[at + 1], LANES - off, 1))
         row = jnp.where(lane < BZ, row, 0.0)
-        out[pl.ds(k, groups, stride=per), :] = pltpu.roll(row, shift, 1)
-
-
-def cut_kernel(counts, rho, mate, *refs):
-    x_sides, y_sides = sides(counts[0]), sides(counts[1])
-    corners = len(x_sides) * len(y_sides)
-    fields, chip, sends = list(refs[:corners]), refs[corners], list(refs[corners + 1 :])
-    cx, cy, _ = position(counts)
-    chip[...] = rho[...] + mate[...]
-    bx = chip.shape[0] // BY
+        chip[pl.ds(k, groups, stride=per), :] = pltpu.roll(row, shift, 1)
+    y, column = grid2(BY, LANES)
+    mine = column % BY == y
+    strips = [jnp.where(mine, flat[3 * groups + x : 3 * groups + x + 1, :], 0.0) for x in range(bx)]
+    chip[...] = chip[...] + wide_dot(jnp.concatenate(strips, 0), z_place(cz))
     for side in x_sides:
         at = pl.multiple_of(BY * rim_start(side, cx, bx, WC), 8)
         sends.pop(0)[...] = chip[pl.ds(at, WC * BY), :].astype(BF16)
@@ -509,12 +531,12 @@
     orb = jnp.transpose(orbitals.reshape(bands, bx, width), (1, 0, 2))
     mate_rows = 2 * flat[0].shape[0] + bx * bands
     inputs = [orb, occupations.reshape(1, bands), *flat]
-    part, orb, mate_block, *x_faces = pl.pallas_call(
+    part, orb, mate_block, weight, *x_faces = pl.pallas_call(
         functools.partial(density_kernel, counts),
         in_specs=[hbm] * 4,
-        out_specs=[vmem()] * (3 + len(x_sides)),
+        out_specs=[vmem()] * (4 + len(x_sides)),
         out_shape=[shape(bx * tiles, LANES), shape(*orb.shape, dtype=BF16)]
-        + [shape(mate_rows, LANES, dtype=BF16)]
+        + [shape(mate_rows, LANES, dtype=BF16), shape(bands, LANES)]
         + [shape(bands, width, dtype=BF16) for _ in x_sides],
         scratch_shapes=[
             pltpu.VMEM((1, bands), F32),
@@ -528,6 +550,14 @@
     )(*(pltpu.with_memory_space_constraint(a, pltpu.HBM) for a in inputs))
     x_faces = [fetch(f, counts, {0: s}) for s, f in zip(x_sides, x_faces)]
     mate_block = fetch(mate_block, counts, {2: "swap"})
+    part = pl.pallas_call(
+        strip_kernel,
+        in_specs=[vmem()] * 3,
+        out_specs=vmem(),
+        out_shape=shape(bx * (tiles + 1), LANES),
+        compiler_params=params(1024),
+        name="strip",
+    )(part, mate_block, weight)
     parts = [part]
     for shift in range(1, groups):
         route = [(i, i ^ shift if groups & (groups - 1) == 0 else (i + shift) % groups) for i in range(groups)]
@@ -559,26 +589,17 @@
     fields = [fetch(r, counts, m) for r, m in zip(rims, moves) if list(m) == [0]]
     fields += [fetch(r, counts, m) for r, m in zip(rims, moves) if list(m) == [1]]
 
-    rho = pl.pallas_call(
-        functools.partial(total_kernel, counts, 1.0 / (bands * groups)),
-        in_specs=[vmem()] * groups,
-        out_specs=vmem(),
-        out_shape=shape(bx * BY, LANES),
-        scratch_shapes=[pltpu.VMEM((bx * tiles, LANES), F32)],
-        compiler_params=params(1024),
-        name="total",
-    )(*parts)
-    mate = fetch(rho, counts, {2: "swap"})
     corner_rows = (WC + 1) * PAD + (WV + WS + 1) * PAD
     cut_rows = [WC * BY] * len(x_sides) + [bx * PAD] * len(y_sides) + [corner_rows] * len(xy_sides)
     chip, *cuts = pl.pallas_call(
-        functools.partial(cut_kernel, counts),
-        in_specs=[vmem()] * (2 + len(corner_rims)),
+        functools.partial(total_kernel, counts, 1.0 / (bands * groups), groups),
+        in_specs=[vmem()] * (groups + len(corner_rims)),
         out_specs=[vmem()] * (1 + len(cut_rows)),
         out_shape=[shape(bx * BY, LANES)] + [shape(n, LANES, dtype=BF16) for n in cut_rows],
+        scratch_shapes=[pltpu.VMEM(part.shape, F32)],
         compiler_params=params(1024),
-        name="cut",
-    )(rho, mate, *corner_rims)
+        name="total",
+    )(*parts, *corner_rims)
     densities = [fetch(c, counts, m) for c, m in zip(cuts, moves)]
 
     rc, ry, qx = BY + 2 * PAD, fy + 2 * PAD, fx + 2 * WV

time: 31.4 us -> 28.2 us (0.90)
  waiting for transfers between devices: 7.23 us -> 1.32 us
  starting transfers between devices: 13.2 us -> 15.8 us
    ppermute x3, waiting for transfers between devices: 3.98 us -> 0.28 us  [step(): parts.append(lax.ppermute(part, 'band', route))]
    ppermute x8 -> x7, starting transfers between devices: 8.77 us -> 11.2 us  [fetch(): return lax.ppermute(block, 'dom', pairs)]
    ppermute x8 -> x7, waiting for transfers between devices: 3.25 us -> 1.03 us  [fetch(): return lax.ppermute(block, 'dom', pairs)]
  transfers between devices with their start and end apart: 11 -> 10, of which waited for: 5 -> 2; matrix products, arithmetic and copies ran while one was open for 0% -> 0% of each run, Pallas kernels for 9% -> 10%
where the time goes in v3:
time: 28.2 us; the launch traced here: 28.1 us
  starting transfers between devices  15.8 us (56%)
  Pallas kernels  10.2 us (36%)
  waiting for transfers between devices  1.32 us (5%)
  between operations  0.71 us (3%)
    ppermute x7, starting transfers between devices, fetch(): return lax.ppermute(block, 'dom', pairs)  11.2 us
    ppermute x3, starting transfers between devices, step(): parts.append(lax.ppermute(part, 'band', route))  4.61 us
    pallas_call x1, Pallas kernels, step(): pl.pallas_call(functools.partial(finish_kernel, counts), in_specs=[vmem()...  4.24 us
    pallas_call x1, Pallas kernels, step(): pl.pallas_call(functools.partial(density_kernel, counts), in_specs=[hbm]...  3.11 us
    pallas_call x1, Pallas kernels, step(): pl.pallas_call(laplace_kernel, in_specs=[vmem()], out_specs=vmem(), out_s...  1.66 us
    ppermute x7, waiting for transfers between devices, fetch(): return lax.ppermute(block, 'dom', pairs)  1.03 us
    pallas_call x1, Pallas kernels, step(): pl.pallas_call(functools.partial(field_kernel, counts), in_specs=[vmem()]...  0.66 us
  transfers between devices with their start and end apart: 10, of which 2 were waited for; matrix products, arithmetic and copies ran while one was open for 0% of the time, Pallas kernels for 10%

profile of v3, /device:TPU:0, one launch (start us, length us, event | category | flops | bytes accessed | tf_op | source)
XLA Modules:
  0.0 28.1 jit_solution(12144506628978601881)
XLA Ops:
  0.6 0.0 copy-start.1
  0.6 0.0 copy-start
  0.7 3.1 %density.1 = (f32[54,128]{1,0:T(8,128)S(1)}, bf16[6,192,1152]{2,1,0:T(8,128)(2,1)S(1)}, bf16[2016,128]{1,0:T(8,128)(2,1)S(1)}, f32[192,128]{1,0:T(8,128)S(1)}, bf16[192,1152]{1,0:T(8,128)(2,1)S(1)}) custom-call(bf16[6,192,1152]{2,1,0:T(8,128)(2,1)} %bitcast.16, f32[1,192]{1,0:T(1,128)} %bitcast.17, f32[432,128]{1,0:T(8,128)} %bitcast.11, f32[432,128]{1,0:T(8,128)} %bitcast.13), custom_call_target="tpu_custom_call" | custom-call | tf_op jit(solution)/shard_map/density/pallas_call | solution.py:534
  3.8 0.6 %collective-permute-start = (bf16[2016,128]{1,0:T(8,128)(2,1)S(1)}, bf16[2016,128]{1,0:T(8,128)(2,1)S(1)}, u32[]{:S(2)}, u32[]{:S(2)}) collective-permute-start(bf16[2016,128]{1,0:T(8,128)(2,1)S(1)} %get-tuple-element.18), channel_id=1, source_target_pairs={{4,0},{0,4},{12,8},{8,12},{20,16},{16,20},{28,24},{24,28},{5,1},{1... | collective-permute-start | bytes 1548296 | tf_op jit(solution)/shard_map/ppermute | solution.py:38
  4.3 2.6 %collective-permute-start.9 = (bf16[192,1152]{1,0:T(8,128)(2,1)S(1)}, bf16[192,1152]{1,0:T(8,128)(2,1)S(1)}, u32[]{:S(2)}, u32[]{:S(2)}) collective-permute-start(bf16[192,1152]{1,0:T(8,128)(2,1)S(1)} %get-tuple-element.29), channel_id=1, source_target_pairs={{16,0},{20,4},{24,8},{28,12},{0,16},{4,20},{8,24},{12,28},{17,1},{... | collective-permute-start | bytes 1327112 | tf_op jit(solution)/shard_map/ppermute | solution.py:38
  6.9 0.0 collective-permute-done.mate.refs_5_
  6.9 0.1 strip.1.refs_0_
  7.0 4.0 %collective-permute-start.3 = (f32[60,128]{1,0:T(8,128)S(1)}, f32[60,128]{1,0:T(8,128)S(1)}, u32[]{:S(2)}, u32[]{:S(2)}) collective-permute-start(f32[60,128]{1,0:T(8,128)S(1)} %strip.1.refs_0_), channel_id=1, source_target_pairs={{0,3},{1,2},{2,1},{3,0},{4,7},{5,6},{6,5},{7,4},{8,11},{9,10},{10,... | collective-permute-start | bytes 92168 | tf_op jit(solution)/shard_map/ppermute | solution.py:564
  11.0 0.0 collective-permute-start.2
  11.0 0.6 %collective-permute-start.1 = (f32[60,128]{1,0:T(8,128)S(1)}, f32[60,128]{1,0:T(8,128)S(1)}, u32[]{:S(2)}, u32[]{:S(2)}) collective-permute-start(f32[60,128]{1,0:T(8,128)S(1)} %strip.1.refs_0_), channel_id=1, source_target_pairs={{0,1},{1,0},{2,3},{3,2},{4,5},{5,4},{6,7},{7,6},{8,9},{9,8},{10,11... | collective-permute-start | bytes 92168 | tf_op jit(solution)/shard_map/ppermute | solution.py:564
  11.6 0.0 copy-done.1
  11.6 0.0 copy-done
  11.6 0.7 %fields.1 = (f32[1152,128]{1,0:T(8,128)S(1)}, bf16[432,128]{1,0:T(8,128)(2,1)S(1)}, bf16[768,128]{1,0:T(8,128)(2,1)S(1)}, bf16[80,128]{1,0:T(8,128)(2,1)S(1)}) custom-call(bf16[6,192,1152]{2,1,0:T(8,128)(2,1)S(1)} %get-tuple-element.20.orb.refs_3_, f32[432,128]{1,0:T(8,128)S(1)} %bitcast.12, f32[432,128]{1,0:T(8,128)S(1)} %bitcast.14, ...), custom_call_target="tpu_custom_call" | custom-call | flops 3000000000 | bytes 1000000 | tf_op jit(solution)/shard_map/fields/pallas_call | solution.py:578
  12.3 1.7 %collective-permute-start.7 = (bf16[432,128]{1,0:T(8,128)(2,1)S(1)}, bf16[432,128]{1,0:T(8,128)(2,1)S(1)}, u32[]{:S(2)}, u32[]{:S(2)}) collective-permute-start(bf16[432,128]{1,0:T(8,128)(2,1)S(1)} %get-tuple-element.27), channel_id=1, source_target_pairs={{16,0},{20,4},{24,8},{28,12},{0,16},{4,20},{8,24},{12,28},{17,1},{... | collective-permute-start | bytes 331784 | tf_op jit(solution)/shard_map/ppermute | solution.py:38
  14.0 0.0 collective-permute-done.3.refs_3_
  14.0 1.5 %collective-permute-start.8 = (bf16[768,128]{1,0:T(8,128)(2,1)S(1)}, bf16[768,128]{1,0:T(8,128)(2,1)S(1)}, u32[]{:S(2)}, u32[]{:S(2)}) collective-permute-start(bf16[768,128]{1,0:T(8,128)(2,1)S(1)} %get-tuple-element.28), channel_id=1, source_target_pairs={{8,0},{12,4},{0,8},{4,12},{24,16},{28,20},{16,24},{20,28},{9,1},{1... | collective-permute-start | bytes 589832 | tf_op jit(solution)/shard_map/ppermute | solution.py:38
  15.5 0.3 collective-permute-done.2.refs_2_
  15.8 0.0 collective-permute-done.1.refs_1_
  15.8 0.2 total.1
  16.0 1.6 %collective-permute-start.5 = (bf16[48,128]{1,0:T(8,128)(2,1)S(1)}, bf16[48,128]{1,0:T(8,128)(2,1)S(1)}, u32[]{:S(2)}, u32[]{:S(2)}) collective-permute-start(bf16[48,128]{1,0:T(8,128)(2,1)S(1)} %get-tuple-element.25), channel_id=1, source_target_pairs={{8,0},{12,4},{0,8},{4,12},{24,16},{28,20},{16,24},{20,28},{9,1},{1... | collective-permute-start | bytes 36872 | tf_op jit(solution)/shard_map/ppermute | solution.py:38
  17.6 1.5 %collective-permute-start.4 = (bf16[72,128]{1,0:T(8,128)(2,1)S(1)}, bf16[72,128]{1,0:T(8,128)(2,1)S(1)}, u32[]{:S(2)}, u32[]{:S(2)}) collective-permute-start(bf16[72,128]{1,0:T(8,128)(2,1)S(1)} %get-tuple-element.24), channel_id=1, source_target_pairs={{16,0},{20,4},{24,8},{28,12},{0,16},{4,20},{8,24},{12,28},{17,1},{... | collective-permute-start | bytes 55304 | tf_op jit(solution)/shard_map/ppermute | solution.py:38
  19.1 0.0 collective-permute-done.9.refs_11_
  19.1 0.0 copy-start.2
  19.1 1.8 %collective-permute-start.6 = (bf16[112,128]{1,0:T(8,128)(2,1)S(1)}, bf16[112,128]{1,0:T(8,128)(2,1)S(1)}, u32[]{:S(2)}, u32[]{:S(2)}) collective-permute-start(bf16[112,128]{1,0:T(8,128)(2,1)S(1)} %get-tuple-element.26), channel_id=1, source_target_pairs={{24,0},{28,4},{16,8},{20,12},{8,16},{12,20},{0,24},{4,28},{25,1},{... | collective-permute-start | bytes 86024 | tf_op jit(solution)/shard_map/ppermute | solution.py:38
  20.9 1.7 %laplace.1.refs_4_ = f32[6,192,1152]{2,1,0:T(8,128)S(1)} custom-call(bf16[6,192,1152]{2,1,0:T(8,128)(2,1)S(1)} %get-tuple-element.20.orb.refs_3_), custom_call_target="tpu_custom_call" | custom-call | flops 6000000000 | bytes 8000000 | tf_op jit(solution)/shard_map/laplace/pallas_call | solution.py:566
  22.5 0.0 copy-done.2
  22.6 0.3 local.1.refs_2_
  22.8 0.0 collective-permute-done.5.refs_7_
  22.8 0.0 collective-permute-done.4.refs_6_
  22.8 1.0 %collective-permute-done.6.refs_8_ = bf16[112,128]{1,0:T(8,128)(2,1)S(1)} collective-permute-done((bf16[112,128]{1,0:T(8,128)(2,1)S(1)}, bf16[112,128]{1,0:T(8,128)(2,1)S(1)}, u32[]{:S(2)}, u32[]{:S(2)}) %collective-permute-start.6) | collective-permute-done | bytes 28704 | tf_op jit(solution)/shard_map/ppermute | solution.py:38
  23.9 0.0 collective-permute-done.7.refs_9_
  23.9 0.0 collective-permute-done.8.refs_10_
  23.9 4.2 %finish.1 = (bf16[6,192,1152]{2,1,0:T(8,128)(2,1)}, f32[432,128]{1,0:T(8,128)}) custom-call(f32[144,128]{1,0:T(8,128)S(1)} %get-tuple-element.22.chip.refs_0_, f32[1152,128]{1,0:T(8,128)S(1)} %get-tuple-element.23.refs_1_, f32[6,1152]{1,0:T(8,128)S(1)} %local.1.refs_2_, bf16[6,192,1152]{2,1,0:T(8,128)(2,1)S(1)} %get-tuple-element.20.orb.refs_3_, ...), custom_call_target="tpu_custom_call" | custom-call | tf_op jit(solution)/shard_map/finish/pallas_call | solution.py:617
Async XLA Ops:
  0.6 11.0 %copy-start.1 = (f32[1,12,4608]{2,0,1:T(1,128)S(1)}, f32[1,12,4608]{2,0,1:T(1,128)}, u32[]{:S(2)}) copy-start(f32[1,12,4608]{2,0,1:T(1,128)} %param.8) | copy-start | bytes 663556
  0.6 11.0 %copy-start = (f32[1,12,4608]{2,0,1:T(1,128)S(1)}, f32[1,12,4608]{2,0,1:T(1,128)}, u32[]{:S(2)}) copy-start(f32[1,12,4608]{2,0,1:T(1,128)} %param.7) | copy-start | bytes 663556
  3.8 3.1 %collective-permute-start = (bf16[2016,128]{1,0:T(8,128)(2,1)S(1)}, bf16[2016,128]{1,0:T(8,128)(2,1)S(1)}, u32[]{:S(2)}, u32[]{:S(2)}) collective-permute-start(bf16[2016,128]{1,0:T(8,128)(2,1)S(1)} %get-tuple-element.18), channel_id=1, source_target_pairs={{4,0},{0,4},{12,8},{8,12},{20,16},{16,20},{28,24},{24,28},{5,1},{1... | collective-permute-start | bytes 1548296 | tf_op jit(solution)/shard_map/ppermute | solution.py:38
  4.3 14.8 %collective-permute-start.9 = (bf16[192,1152]{1,0:T(8,128)(2,1)S(1)}, bf16[192,1152]{1,0:T(8,128)(2,1)S(1)}, u32[]{:S(2)}, u32[]{:S(2)}) collective-permute-start(bf16[192,1152]{1,0:T(8,128)(2,1)S(1)} %get-tuple-element.29), channel_id=1, source_target_pairs={{16,0},{20,4},{24,8},{28,12},{0,16},{4,20},{8,24},{12,28},{17,1},{... | collective-permute-start | bytes 1327112 | tf_op jit(solution)/shard_map/ppermute | solution.py:38
  7.0 7.0 %collective-permute-start.3 = (f32[60,128]{1,0:T(8,128)S(1)}, f32[60,128]{1,0:T(8,128)S(1)}, u32[]{:S(2)}, u32[]{:S(2)}) collective-permute-start(f32[60,128]{1,0:T(8,128)S(1)} %strip.1.refs_0_), channel_id=1, source_target_pairs={{0,3},{1,2},{2,1},{3,0},{4,7},{5,6},{6,5},{7,4},{8,11},{9,10},{10,... | collective-permute-start | bytes 92168 | tf_op jit(solution)/shard_map/ppermute | solution.py:564
  11.0 4.8 %collective-permute-start.2 = (f32[60,128]{1,0:T(8,128)S(1)}, f32[60,128]{1,0:T(8,128)S(1)}, u32[]{:S(2)}, u32[]{:S(2)}) collective-permute-start(f32[60,128]{1,0:T(8,128)S(1)} %strip.1.refs_0_), channel_id=1, source_target_pairs={{0,2},{1,3},{2,0},{3,1},{4,6},{5,7},{6,4},{7,5},{8,10},{9,11},{10,... | collective-permute-start | bytes 92168 | tf_op jit(solution)/shard_map/ppermute | solution.py:564
  11.0 4.8 %collective-permute-start.1 = (f32[60,128]{1,0:T(8,128)S(1)}, f32[60,128]{1,0:T(8,128)S(1)}, u32[]{:S(2)}, u32[]{:S(2)}) collective-permute-start(f32[60,128]{1,0:T(8,128)S(1)} %strip.1.refs_0_), channel_id=1, source_target_pairs={{0,1},{1,0},{2,3},{3,2},{4,5},{5,4},{6,7},{7,6},{8,9},{9,8},{10,11... | collective-permute-start | bytes 92168 | tf_op jit(solution)/shard_map/ppermute | solution.py:564
  12.3 11.6 %collective-permute-start.7 = (bf16[432,128]{1,0:T(8,128)(2,1)S(1)}, bf16[432,128]{1,0:T(8,128)(2,1)S(1)}, u32[]{:S(2)}, u32[]{:S(2)}) collective-permute-start(bf16[432,128]{1,0:T(8,128)(2,1)S(1)} %get-tuple-element.27), channel_id=1, source_target_pairs={{16,0},{20,4},{24,8},{28,12},{0,16},{4,20},{8,24},{12,28},{17,1},{... | collective-permute-start | bytes 331784 | tf_op jit(solution)/shard_map/ppermute | solution.py:38
  14.0 9.9 %collective-permute-start.8 = (bf16[768,128]{1,0:T(8,128)(2,1)S(1)}, bf16[768,128]{1,0:T(8,128)(2,1)S(1)}, u32[]{:S(2)}, u32[]{:S(2)}) collective-permute-start(bf16[768,128]{1,0:T(8,128)(2,1)S(1)} %get-tuple-element.28), channel_id=1, source_target_pairs={{8,0},{12,4},{0,8},{4,12},{24,16},{28,20},{16,24},{20,28},{9,1},{1... | collective-permute-start | bytes 589832 | tf_op jit(solution)/shard_map/ppermute | solution.py:38
  16.0 6.8 %collective-permute-start.5 = (bf16[48,128]{1,0:T(8,128)(2,1)S(1)}, bf16[48,128]{1,0:T(8,128)(2,1)S(1)}, u32[]{:S(2)}, u32[]{:S(2)}) collective-permute-start(bf16[48,128]{1,0:T(8,128)(2,1)S(1)} %get-tuple-element.25), channel_id=1, source_target_pairs={{8,0},{12,4},{0,8},{4,12},{24,16},{28,20},{16,24},{20,28},{9,1},{1... | collective-permute-start | bytes 36872 | tf_op jit(solution)/shard_map/ppermute | solution.py:38
  17.6 5.3 %collective-permute-start.4 = (bf16[72,128]{1,0:T(8,128)(2,1)S(1)}, bf16[72,128]{1,0:T(8,128)(2,1)S(1)}, u32[]{:S(2)}, u32[]{:S(2)}) collective-permute-start(bf16[72,128]{1,0:T(8,128)(2,1)S(1)} %get-tuple-element.24), channel_id=1, source_target_pairs={{16,0},{20,4},{24,8},{28,12},{0,16},{4,20},{8,24},{12,28},{17,1},{... | collective-permute-start | bytes 55304 | tf_op jit(solution)/shard_map/ppermute | solution.py:38
  19.1 3.5 %copy-start.2 = (f32[1,6,1152]{2,0,1:T(1,128)S(1)}, f32[1,6,1152]{2,0,1:T(1,128)}, u32[]{:S(2)}) copy-start(f32[1,6,1152]{2,0,1:T(1,128)} %param.9) | copy-start | bytes 82948
  19.1 4.8 %collective-permute-start.6 = (bf16[112,128]{1,0:T(8,128)(2,1)S(1)}, bf16[112,128]{1,0:T(8,128)(2,1)S(1)}, u32[]{:S(2)}, u32[]{:S(2)}) collective-permute-start(bf16[112,128]{1,0:T(8,128)(2,1)S(1)} %get-tuple-element.26), channel_id=1, source_target_pairs={{24,0},{28,4},{16,8},{20,12},{8,16},{12,20},{0,24},{4,28},{25,1},{... | collective-permute-start | bytes 86024 | tf_op jit(solution)/shard_map/ppermute | solution.py:38
